TPU v7x, 32 devices: a whole 2x2x4 slice. The times are simulated.
32 devices in a mesh: dp: 4 (over x, y), tp: 8 (over z, core).
Axes of the slice: x: 2, y: 2, z: 4, core: 2. Of those that a mesh axis runs over, the one named last changes fastest.
Arguments:
- x_in: bfloat16 [8, 2048, 2048], P('dp'), parts along dimension 0
- start_pos: int32 [8], P('dp'), parts along dimension 0
- kv_state: float32 [8, 8, 256, 512], P('dp', 'tp'), parts along dimension 0
- ln1_gain: float32 [2048], replicated
- ln1_bias: float32 [2048], replicated
- w_q: bfloat16 [2048, 2048], P(None, 'tp')
- w_k: bfloat16 [2048, 2048], P(None, 'tp')
- w_v: bfloat16 [2048, 4096], P(None, 'tp')
- w_g: bfloat16 [2048, 4096], P(None, 'tp')
- w_o: bfloat16 [4096, 2048], P('tp')
- ln2_gain: float32 [2048], replicated
- ln2_bias: float32 [2048], replicated
- w_up: bfloat16 [2048, 4096], P(None, 'tp')
- w_down: bfloat16 [4096, 2048], P('tp')
Outputs:
- output 1: bfloat16 [8, 2048, 2048], P('dp'), parts along dimension 0
- output 2: float32 [8, 8, 256, 512], P('dp', 'tp'), parts along dimension 0
There are 4 independent parts. A program takes and returns all parts, laid end to end along the dimension named above; an argument that names none is the same for every part.
All inputs are finite; a program needn't handle non-finite values.
Results may differ from a plain program's by a relative error of at most 0.0145129.
Values are sent between devices in bfloat16 or wider.
A program may use at most 1 GiB of HBM per device.

v0:
```python
import jax
import jax.numpy as jnp
from jax import lax
from jax.sharding import PartitionSpec as P

NORM_EPS = 1e-5
GROUP_EPS = 1e-6
ROPE_BASE = 10000.0


def layer_norm(x_f32, norm_gain, norm_bias):
    row_mean = jnp.mean(x_f32, axis=-1, keepdims=True)
    centered = x_f32 - row_mean
    variance = jnp.mean(centered * centered, axis=-1, keepdims=True)
    return centered * lax.rsqrt(variance + NORM_EPS) * norm_gain + norm_bias


def rotate_half(head_vecs, cos_t, sin_t):
    half_dim = head_vecs.shape[-1] // 2
    first_half = head_vecs[..., :half_dim]
    second_half = head_vecs[..., half_dim:]
    return jnp.concatenate([first_half * cos_t - second_half * sin_t, second_half * cos_t + first_half * sin_t], axis=-1)


def rope_tables(first_pos, chunk_len, key_dim):
    half_dim = key_dim // 2
    inv_freq = jnp.power(ROPE_BASE, -jnp.arange(half_dim).astype(jnp.float32) / half_dim)
    positions = (first_pos[:, None] + jnp.arange(chunk_len)[None, :]).astype(jnp.float32)
    angles = positions[:, :, None] * inv_freq
    return jnp.cos(angles)[:, :, None, :], jnp.sin(angles)[:, :, None, :]


def head_log_decay(head_ids):
    return jnp.log1p(-jnp.exp2(-5.0 - head_ids.astype(jnp.float32)))


def project_heads(h_one, cos_t, sin_t, w_q, w_k, w_v, w_g, num_heads):
    d_model = h_one.shape[-1]
    key_dim = w_q.shape[1] // num_heads
    val_dim = w_v.shape[1] // num_heads
    q_raw = jnp.einsum('bcd,dhk->bchk', h_one, w_q.reshape(d_model, num_heads, key_dim), preferred_element_type=jnp.float32)
    k_raw = jnp.einsum('bcd,dhk->bchk', h_one, w_k.reshape(d_model, num_heads, key_dim), preferred_element_type=jnp.float32)
    queries = rotate_half(q_raw, cos_t, sin_t).astype(jnp.bfloat16)
    keys = (rotate_half(k_raw, cos_t, sin_t) * key_dim ** -0.5).astype(jnp.bfloat16)
    values = jnp.einsum('bcd,dhe->bche', h_one, w_v.reshape(d_model, num_heads, val_dim), preferred_element_type=jnp.float32).astype(jnp.bfloat16)
    gates = jnp.einsum('bcd,dhe->bche', h_one, w_g.reshape(d_model, num_heads, val_dim), preferred_element_type=jnp.float32)
    return queries, keys, values, gates


def mix_heads(queries, keys, values_f32, gates, state_in, log_gamma, w_o):
    chunk_len = queries.shape[1]
    num_heads = queries.shape[2]
    val_dim = values_f32.shape[3]
    step_ids = jnp.arange(chunk_len)
    step_gap = step_ids[:, None] - step_ids[None, :]
    inner_decay = jnp.where(step_gap[None] >= 0, jnp.exp(jnp.maximum(step_gap, 0).astype(jnp.float32)[None] * log_gamma[:, None, None]), 0.0)
    query_decay = jnp.exp((step_ids + 1).astype(jnp.float32)[:, None] * log_gamma[None, :])
    scores = jnp.einsum('bchk,bjhk->bhcj', queries, keys, preferred_element_type=jnp.float32) * inner_decay
    retained = jnp.einsum('bhcj,bjhe->bche', scores, values_f32) + jnp.einsum('bchk,bhke->bche', queries.astype(jnp.float32), state_in) * query_decay[:, :, None]
    row_mean = jnp.mean(retained, axis=-1, keepdims=True)
    centered = retained - row_mean
    variance = jnp.mean(centered * centered, axis=-1, keepdims=True)
    normed = centered * lax.rsqrt(variance + GROUP_EPS)
    mixed = (jax.nn.silu(gates) * normed).astype(jnp.bfloat16)
    return jnp.einsum('bche,hed->bcd', mixed, w_o.reshape(num_heads, val_dim, w_o.shape[1]), preferred_element_type=jnp.float32)


def chunk_state(keys, values_f32, log_gamma):
    chunk_len = keys.shape[1]
    step_ids = jnp.arange(chunk_len)
    key_decay = jnp.exp((chunk_len - 1 - step_ids).astype(jnp.float32)[:, None] * log_gamma[None, :])
    return jnp.einsum('bjhk,bjhe->bhke', keys.astype(jnp.float32) * key_decay[:, :, None], values_f32)


def feed_forward(x_mid, ln2_gain, ln2_bias, w_up, w_down):
    h_two = layer_norm(x_mid.astype(jnp.float32), ln2_gain, ln2_bias).astype(jnp.bfloat16)
    activated = jax.nn.gelu(jnp.einsum('bcd,df->bcf', h_two, w_up, preferred_element_type=jnp.float32), approximate=False).astype(jnp.bfloat16)
    return jnp.einsum('bcf,fd->bcd', activated, w_down, preferred_element_type=jnp.float32)


def solution(mesh):
    def local_layer(x_in, start_pos, kv_state, ln1_gain, ln1_bias, w_q, w_k, w_v, w_g, w_o, ln2_gain, ln2_bias, w_up, w_down):
        local_heads = kv_state.shape[1]
        chunk_len = x_in.shape[1]
        head_ids = lax.axis_index('tp') * local_heads + jnp.arange(local_heads)
        log_gamma = head_log_decay(head_ids)
        x_f32 = x_in.astype(jnp.float32)
        h_one = layer_norm(x_f32, ln1_gain, ln1_bias).astype(jnp.bfloat16)
        cos_t, sin_t = rope_tables(start_pos, chunk_len, kv_state.shape[2])
        queries, keys, values, gates = project_heads(h_one, cos_t, sin_t, w_q, w_k, w_v, w_g, local_heads)
        values_f32 = values.astype(jnp.float32)
        attn_part = mix_heads(queries, keys, values_f32, gates, kv_state, log_gamma, w_o).astype(jnp.bfloat16)
        new_state = jnp.exp(chunk_len * log_gamma)[:, None, None] * kv_state + chunk_state(keys, values_f32, log_gamma)
        attn_out = lax.psum(attn_part, 'tp')
        x_mid = (x_f32 + attn_out.astype(jnp.float32)).astype(jnp.bfloat16)
        ffn_part = feed_forward(x_mid, ln2_gain, ln2_bias, w_up, w_down).astype(jnp.bfloat16)
        ffn_out = lax.psum(ffn_part, 'tp')
        x_out = (x_mid.astype(jnp.float32) + ffn_out.astype(jnp.float32)).astype(jnp.bfloat16)
        return x_out, new_state

    in_specs = (P('dp', None, None), P('dp'), P('dp', 'tp', None, None), P(), P(), P(None, 'tp'), P(None, 'tp'), P(None, 'tp'), P(None, 'tp'), P('tp', None), P(), P(), P(None, 'tp'), P('tp', None))
    out_specs = (P('dp', None, None), P('dp', 'tp', None, None))
    return jax.shard_map(local_layer, mesh=mesh, in_specs=in_specs, out_specs=out_specs, check_vma=False)
```

profile of v0, /device:TPU:0, one launch (start us, length us, event | category | flops | bytes accessed | tf_op | source)
XLA Modules:
  0.0 900.2 jit_solution(14664558261698258055)
XLA Ops:
  7.2 0.0 copy-start
  7.2 0.0 all-reduce.3.cloned.1.call-start
  7.3 0.0 copy-start.9
  7.4 0.0 copy-start.3
  7.4 11.3 %exponential_select_fusion = f32[2048,2048]{1,0:T(8,128)} fusion(f32[]{:T(128)S(6)} %log1p.4), kind=kLoop, calls=%fused_computation.28 | loop fusion | flops 25165824 | bytes 16777220 | tf_op jit(solution)/shard_map/jit(_where)/select_n | solution.py:56
  18.6 0.0 copy-done.9
  18.6 0.1 add_convert_fusion
  18.7 0.0 copy-done.3
  18.7 3.0 convert_reduce_fusion.1
  21.8 0.0 copy-start.10
  21.8 0.0 copy-start.13
  21.8 0.0 copy-start.14
  21.8 5.5 fusion.8
  27.3 0.0 copy-done.10
  27.3 0.0 copy-done.13
  27.3 0.0 copy-done.14
  27.3 0.0 copy-start.11
  27.4 14.8 %convolution_convert_fusion.2 = bf16[2,2048,512]{2,1,0:T(8,128)(2,1)} fusion(bf16[2048,512]{1,0:T(8,128)(2,1)S(1)} %copy-done.10, bf16[2,2048,2048]{2,1,0:T(8,128)(2,1)} %param.14, f32[2048]{0:T(1024)S(1)} %copy-done.13, f32[2048]{0:T(1024)S(1)} %copy-done.14, f32[2,2048]{1,0:T(2,128)S(1)} %add_rsqrt_fusion.2, f32[2,2048]{1,0:T(2,128)S(1)} %broadcast_multiply_fusion.2), kind=kOutput, calls=%fused_computation.99 | convolution fusion | flops 8642363392 | bytes 23117824 | tf_op jit(solution)/shard_map/bcd,dhe->bche/dot_general | solution.py:45
  42.1 0.0 copy-done.11
  42.1 0.0 copy-start.12
  42.1 10.8 %convolution_bitcast_fusion.1 = f32[2,2048,1,256]{1,3,0,2:T(8,128)S(1)} fusion(bf16[2048,256]{1,0:T(8,128)(2,1)S(1)} %copy-done.11, bf16[2,2048,2048]{2,1,0:T(8,128)(2,1)} %param.14, f32[2048]{0:T(1024)S(1)} %copy-done.13, f32[2048]{0:T(1024)S(1)} %copy-done.14, f32[2,2048]{1,0:T(2,128)S(1)} %add_rsqrt_fusion.2, f32[2,2048]{1,0:T(2,128)S(1)} %broadcast_multiply_fusion.2), kind=kOutput, calls=%fused_computation.101 | convolution fusion | flops 4345298944 | bytes 22069248 | tf_op jit(solution)/shard_map/bcd,dhk->bchk/dot_general | solution.py:41
  53.0 0.0 copy-done.12
  53.0 10.8 %convolution_bitcast_fusion = f32[2,2048,1,256]{1,3,0,2:T(8,128)S(1)} fusion(bf16[2048,256]{1,0:T(8,128)(2,1)S(1)} %copy-done.12, bf16[2,2048,2048]{2,1,0:T(8,128)(2,1)} %param.14, f32[2048]{0:T(1024)S(1)} %copy-done.13, f32[2048]{0:T(1024)S(1)} %copy-done.14, f32[2,2048]{1,0:T(2,128)S(1)} %add_rsqrt_fusion.2, f32[2,2048]{1,0:T(2,128)S(1)} %broadcast_multiply_fusion.2), kind=kOutput, calls=%fused_computation.100 | convolution fusion | flops 4345298944 | bytes 22069248 | tf_op jit(solution)/shard_map/bcd,dhk->bchk/dot_general | solution.py:42
  63.8 0.0 copy-start.7
  63.8 9.9 %fusion.90 = (f32[2,2048,128]{1,2,0:T(8,128)}, f32[2,2048,128]{1,2,0:T(8,128)}, bf16[2,2048,128]{1,2,0:T(8,128)(2,1)S(1)}, bf16[2,2048,128]{1,2,0:T(8,128)(2,1)S(1)}) fusion(f32[2,2048,1,256]{1,3,0,2:T(8,128)S(1)} %convolution_bitcast_fusion, f32[128]{0:T(128)S(1)} %multiply_power_fusion, f32[2,2048]{1,0:T(2,128)S(1)} %add_convert_fusion, ...), kind=kLoop, calls=%fused_computation.117 | loop fusion | flops 7864320 | bytes 14696960 | tf_op jit(solution)/shard_map/concatenate | solution.py:22
  73.7 0.0 copy-start.5
  73.7 1.0 copy-done.5
  74.7 0.0 copy-done.7
  74.7 4.5 fusion.104
  79.2 26.0 %fusion.167 = (f32[2,2048]{1,0:T(2,128)S(1)}, f32[2,2048,1,512]{3,1,0,2:T(8,128)}) fusion(f32[2048]{0:T(1024)S(1)} %multiply_exponential_fusion.1, f32[2,2048,512]{2,1,0:T(8,128)} %fusion.104, bf16[2,2048,512]{2,1,0:T(8,128)(2,1)} %convolution_convert_fusion.2, f32[2048,2048]{1,0:T(8,128)} %exponential_select_fusion, ...), kind=kOutput, calls=%fused_computation.188 | convolution fusion | flops 12906917888 | bytes 44064768 | tf_op jit(solution)/shard_map/bhcj,bjhe->bche/dot_general | solution.py:59
  105.2 0.0 copy-start.4
  105.2 4.3 multiply_reduce_fusion
  109.5 1.5 copy-done.4
  111.0 14.0 %fusion.31 = bf16[2,2048,1,512]{3,1,0,2:T(8,128)(2,1)S(1)} fusion(f32[2,2048,1,512]{3,1,0,2:T(8,128)S(1)} %copy-done.4, f32[2,2048]{1,0:T(2,128)S(1)} %add_rsqrt_fusion.1, f32[2,2048]{1,0:T(2,128)S(1)} %broadcast_multiply_fusion, bf16[2048,512]{1,0:T(8,128)(2,1)} %param.22, bf16[2,2048,2048]{2,1,0:T(8,128)(2,1)} %param.14, f32[2048]{0:T(1024)S(1)} %copy-done.13, ...), kind=kOutput, calls=%fused_computation.47 | convolution fusion | flops 8657043456 | bytes 31539200 | tf_op jit(solution)/shard_map/bcd,dhe->bche/dot_general | solution.py:46
  125.0 0.0 copy-done
  125.0 11.9 %convolution_convert_fusion.1 = bf16[2,2048,2048]{2,1,0:T(8,128)(2,1)} fusion(bf16[2,2048,1,512]{3,1,0,2:T(8,128)(2,1)S(1)} %fusion.31, bf16[512,2048]{1,0:T(8,128)(2,1)S(1)} %copy-done), kind=kOutput, calls=%fused_computation.34 | convolution fusion | flops 8598323200 | bytes 23068672 | tf_op jit(solution)/shard_map/bche,hed->bcd/dot_general | solution.py:65
  136.9 0.0 all-reduce.3.cloned.1.call-update
  137.0 0.0 all-reduce.5.cloned.1.call-start
  137.0 335.5 %all-reduce.3.cloned.1.call-done = bf16[2,2048,2048]{2,1,0:T(8,128)(2,1)} async-done(((bf16[2,2048,2048]{2,1,0:T(8,128)(2,1)}), bf16[2,2048,2048]{2,1,0:T(8,128)(2,1)}) %all-reduce.3.cloned.1.call-update) | async-done | bytes 16777232 | tf_op jit(solution)/shard_map/psum | solution.py:94
  472.5 13.8 %convert_reduce_fusion = (f32[2,2048]{1,0:T(2,128)S(1)}, bf16[2,2048,2048]{2,1,0:T(8,128)(2,1)S(1)}) fusion(bf16[2,2048,2048]{2,1,0:T(8,128)(2,1)} %all-reduce.3.cloned.1.call-done, bf16[2,2048,2048]{2,1,0:T(8,128)(2,1)} %param.14), kind=kLoop, calls=%fused_computation.2 | loop fusion | flops 50327552 | bytes 50348032 | tf_op jit(solution)/shard_map/reduce_sum | solution.py:12
  486.2 0.0 copy-start.2
  486.3 0.0 copy-start.15
  486.3 0.0 copy-start.16
  486.3 5.5 fusion.4
  491.8 0.6 copy-done.2
  492.4 0.0 copy-done.15
  492.4 0.0 copy-done.16
  492.4 16.6 %fusion.100 = (u8[2048,512]{1,0:T(8,128)(4,1)S(1)}, u8[2048,512]{1,0:T(8,128)(4,1)}, f32[2,2048,512]{2,1,0:T(8,128)}) fusion(bf16[2048,512]{1,0:T(8,128)(2,1)} %param.26, bf16[2,2048,2048]{2,1,0:T(8,128)(2,1)S(1)} %get-tuple-element.7, f32[2048]{0:T(1024)S(1)} %copy-done.15, f32[2048]{0:T(1024)S(1)} %copy-done.16, f32[2,2048]{1,0:T(2,128)S(1)} %add_rsqrt_fusion, ...), kind=kOutput, calls=%fused_computation.128 | convolution fusion | flops 8665432064 | bytes 29409280 | tf_op jit(solution)/shard_map/bcd,df->bcf/dot_general | solution.py:77
  509.0 31.1 %convolution_convert_fusion = bf16[2,2048,2048]{2,1,0:T(8,128)(2,1)} fusion(f32[2,2048,512]{2,1,0:T(8,128)} %get-tuple-element.16, bf16[512,2048]{1,0:T(8,128)(2,1)} %param.27, u8[2048,512]{1,0:T(8,128)(4,1)} %get-tuple-element.5, u8[2048,512]{1,0:T(8,128)(4,1)S(1)} %get-tuple-element.4), kind=kOutput, calls=%fused_computation.33 | convolution fusion | flops 8745123840 | bytes 29360128 | tf_op jit(solution)/shard_map/bcf,fd->bcd/dot_general | solution.py:78
  540.1 0.0 copy-start.6
  540.1 0.0 copy-start.8
  540.1 0.0 all-reduce.5.cloned.1.call-update
  540.2 1.5 copy-done.6
  541.7 0.3 copy-done.8
  541.9 5.1 fusion.108
  547.0 326.0 %all-reduce.5.cloned.1.call-done = bf16[2,2048,2048]{2,1,0:T(8,128)(2,1)} async-done(((bf16[2,2048,2048]{2,1,0:T(8,128)(2,1)}), bf16[2,2048,2048]{2,1,0:T(8,128)(2,1)}) %all-reduce.5.cloned.1.call-update) | async-done | bytes 16777232 | tf_op jit(solution)/shard_map/psum | solution.py:97
  873.0 0.0 copy-start.1
  873.0 19.9 %fusion.13 = bf16[2,2048,2048]{2,1,0:T(8,128)(2,1)} fusion(bf16[2,2048,2048]{2,1,0:T(8,128)(2,1)} %copy-done.2, bf16[2,2048,2048]{2,1,0:T(8,128)(2,1)} %all-reduce.5.cloned.1.call-done), kind=kLoop, calls=%fused_computation.19 | loop fusion | flops 33554432 | bytes 50331648 | tf_op jit(solution)/shard_map/convert_element_type | solution.py:98
  892.9 0.0 copy-done.1
  (9 shorter events, 0.1 us)
Async XLA Ops:
  7.2 117.8 %copy-start = (bf16[512,2048]{1,0:T(8,128)(2,1)S(1)}, bf16[512,2048]{1,0:T(8,128)(2,1)}, u32[]{:S(2)}) copy-start(bf16[512,2048]{1,0:T(8,128)(2,1)} %param.23) | copy-start | bytes 6291460
  7.2 465.3 %all-reduce.3.cloned.1.call-start = ((), (), s32[]{:S(2)}) async-start(), calls=%async_computation | async-start | bytes 33554432 | tf_op jit(solution)/shard_map/psum | solution.py:94
  7.3 11.3 %copy-start.9 = (s32[2]{0:T(128)S(1)}, s32[2]{0:T(128)}, u32[]{:S(2)}) copy-start(s32[2]{0:T(128)} %param.15) | copy-start | bytes 28
  7.4 11.4 %copy-start.3 = (bf16[2,2048,2048]{2,1,0:T(8,128)(2,1)S(1)}, bf16[2,2048,2048]{2,1,0:T(8,128)(2,1)}, u32[]{:S(2)}) copy-start(bf16[2,2048,2048]{2,1,0:T(8,128)(2,1)} %param.14) | copy-start | bytes 50331652
  21.8 5.5 copy-start.10
  21.8 5.5 copy-start.13
  21.8 5.5 copy-start.14
  27.3 14.8 %copy-start.11 = (bf16[2048,256]{1,0:T(8,128)(2,1)S(1)}, bf16[2048,256]{1,0:T(8,128)(2,1)}, u32[]{:S(2)}) copy-start(bf16[2048,256]{1,0:T(8,128)(2,1)} %param.19) | copy-start | bytes 3145732
  42.1 10.8 %copy-start.12 = (bf16[2048,256]{1,0:T(8,128)(2,1)S(1)}, bf16[2048,256]{1,0:T(8,128)(2,1)}, u32[]{:S(2)}) copy-start(bf16[2048,256]{1,0:T(8,128)(2,1)} %param.20) | copy-start | bytes 3145732
  63.8 10.9 %copy-start.7 = (f32[2,1,256,512]{3,2,1,0:T(8,128)S(1)}, f32[2,1,256,512]{3,2,1,0:T(8,128)}, u32[]{:S(2)}) copy-start(f32[2,1,256,512]{3,2,1,0:T(8,128)} %param.16) | copy-start | bytes 3145732
  73.7 1.0 copy-start.5
  105.2 5.8 copy-start.4
  137.0 736.0 %all-reduce.5.cloned.1.call-start = ((), (), s32[]{:S(2)}) async-start(), calls=%async_computation.1 | async-start | bytes 33554432 | tf_op jit(solution)/shard_map/psum | solution.py:97
  486.2 6.2 copy-start.2
  486.3 6.1 copy-start.15
  486.3 6.1 copy-start.16
  540.1 1.6 copy-start.6
  540.1 1.9 copy-start.8
  873.0 19.9 %copy-start.1 = (bf16[512,2048]{1,0:T(8,128)(2,1)S(1)}, bf16[512,2048]{1,0:T(8,128)(2,1)}, u32[]{:S(2)}) copy-start(bf16[512,2048]{1,0:T(8,128)(2,1)} %param.23) | copy-start | bytes 6291460
Sparse Core Ops, SparseCore 0:
  137.1 335.3 all-reduce.2
  540.2 332.7 all-reduce.4
where the time goes:
time: 903 us; the launch traced here: 900 us
  waiting for transfers between devices  661 us (73%)
  matrix products  146 us (16%)
  other arithmetic  73.3 us (8%)
  between operations  14.9 us (2%)
    psum x1, waiting for transfers between devices, local_layer(): attn_out = lax.psum(attn_part, 'tp')  335 us
    psum x1, waiting for transfers between devices, local_layer(): ffn_out = lax.psum(ffn_part, 'tp')  326 us
    dot_general x1, matrix products, feed_forward(): jnp.einsum('bcf,fd->bcd', activated, w_down, preferred_element_type=jnp.f...  31.1 us
    dot_general x1, matrix products, mix_heads(): jnp.einsum('bhcj,bjhe->bche', scores, values_f32)  26 us
    convert_element_type x1, other arithmetic, local_layer(): (x_mid.astype(jnp.float32) + ffn_out.astype(jnp.float32)).astype(jnp.bflo...  19.9 us
  transfers between devices with their start and end apart: 2, of which 2 were waited for; matrix products, arithmetic and copies ran while one was open for 1% of the time, Pallas kernels for 0%

commit v1 on v0

v1 whole, which is shorter than its diff:
```python
import jax
import jax.numpy as jnp
from jax import lax
from jax.experimental import pallas as pl
from jax.experimental.pallas import tpu as pltpu
from jax.sharding import PartitionSpec as P

NORM_EPS = 1e-5
GROUP_EPS = 1e-6
ROPE_BASE = 10000.0
CHUNK = 256
BLOCKS = 4
CHIPS = 4
F32 = jnp.float32
BF16 = jnp.bfloat16
MESH = pl.DeviceIdType.MESH


def normalize(x_f32, gain, bias):
    row_mean = jnp.mean(x_f32, axis=-1, keepdims=True)
    centered = x_f32 - row_mean
    variance = jnp.mean(centered * centered, axis=-1, keepdims=True)
    return centered * lax.rsqrt(variance + NORM_EPS) * gain + bias


def add_bf16(*terms):
    return sum(t.astype(F32) for t in terms).astype(BF16)


def layer_kernel(x_any, state_in, gain1, bias1, gain2, bias2, wq_any, wk_any, wv_any, wg_any, wo_any, up_any, down_any, base, table, decay, edge,
                 out_any, state_ref, up_all, down_all,
                 wq, wk, wv, wg, wo, wd, x_buf, part, met, own, rs, mid, hid, acc,
                 load_sem, x_sem, mid_sem, tile_sem, met_s, met_r, credit, rs_s, rs_r, z_s, z_r, f_s, f_r, g_s, g_r, p_s, p_r, ag_s, ag_r, agp_s, agp_r, put_sem):
    group, me = lax.axis_index('dp'), lax.axis_index('tp')
    chip, core = lax.div(me, 2), lax.rem(me, 2)
    partner = me + 1 - 2 * core
    across_x = lax.rem(group + 2, 4)
    across_y = group + 1 - 2 * lax.rem(group, 2)
    chunk = decay.shape[0]
    rows, share = own.shape[1], mid.shape[1]
    key_dim, half = wq.shape[1], wq.shape[1] // 2
    last = CHIPS - 1

    def remote(src, dst, s, r, **where):
        return pltpu.make_async_remote_copy(src_ref=src, dst_ref=dst, send_sem=s, recv_sem=r, device_id=where, device_id_type=MESH)

    weight_all, weight_own = (up_all, down_all), (up_any, down_any)
    quarter = tuple(w.shape[0] // 4 for w in weight_own)

    def piece(p, shard, q):
        return weight_all[p].at[shard, pl.ds(q * quarter[p], quarter[p])]

    def z_copy(side, hop, p):
        origin = chip - hop if side == 0 else chip + hop
        slot = piece(p, 2 * origin + core, group)
        src = weight_own[p].at[pl.ds(group * quarter[p], quarter[p])] if hop == 0 else slot
        return remote(src, slot, z_s.at[side, hop, p], z_r.at[origin, p], tp=me + 2 if side == 0 else me - 2)

    def first_copy(axis, origin, p, q=None):
        slot = piece(p, 2 * origin + core, group if q is None else q)
        return remote(slot, slot, f_s.at[axis, origin, p], f_r.at[axis, origin, p], dp=across_x if axis == 0 else across_y)

    def second_copy(origin, p, q=None):
        slot = piece(p, 2 * origin + core, (across_x if p == 0 else across_y) if q is None else q)
        return remote(slot, slot, g_s.at[origin, p], g_r.at[origin, p], dp=across_y if p == 0 else across_x)

    def partner_copy(origin, p, own_shard=False, incoming=False):
        slot = weight_all[p].at[2 * origin + (1 - core if incoming else core)]
        return remote(weight_own[p] if own_shard else slot, slot, p_s.at[origin, p], p_r.at[origin, p], tp=partner)

    def sides(d):
        return ((0, chip - d, chip >= d, chip < last), (1, chip + d, chip + d <= last, chip > 0))

    def spread_first(d):
        for side, origin, valid, onward in sides(d):
            @pl.when(valid)
            def _():
                for p in range(2):
                    remote(piece(p, 2 * origin + core, group), piece(p, 2 * origin + core, group), z_s.at[side, d - 1, p], z_r.at[origin, p], tp=partner).wait_recv()
                if d < last:
                    @pl.when(onward)
                    def _():
                        for p in range(2):
                            z_copy(side, d, p).start()
                for p in range(2):
                    for axis in range(2):
                        first_copy(axis, origin, p).start()

    def spread_second(d):
        for side, origin, valid, onward in sides(d):
            @pl.when(valid)
            def _():
                for p in range(2):
                    first_copy(0, origin, p, across_x).wait_recv()
                    first_copy(1, origin, p, across_y).wait_recv()
                for p in range(2):
                    second_copy(origin, p).start()

    def spread_third(d):
        for side, origin, valid, onward in sides(d):
            @pl.when(valid)
            def _():
                for p in range(2):
                    second_copy(origin, p, 3 - group).wait_recv()
                for p in range(2):
                    partner_copy(origin, p).start()

    def rs_copy(side, i, t, fresh):
        k = lax.rem(chip + (CHIPS - t if side == 0 else t), CHIPS)
        src = own.at[i, pl.ds(k * share, share)] if fresh else rs.at[side, i, t - 2]
        return remote(src, rs.at[side, i, t - 1], rs_s.at[side, i, t - 1], rs_r.at[side, i, t - 1], tp=me + 2 if side == 0 else me - 2)

    def rs_first(i):
        for side, end in ((0, 0), (1, last)):
            @pl.when(chip == end)
            def _():
                for t in range(1, CHIPS):
                    rs_copy(side, i, t, True).start()

    def rs_senders(side, t):
        return (chip >= 1) & (chip <= t - 1) & (chip < last) if side == 0 else (chip < last) & (chip >= CHIPS - t) & (chip >= 1)

    def rs_step(i, t):
        for side in range(2):
            @pl.when(rs_senders(side, t))
            def _():
                rs_copy(side, i, t - 1, False if t > 2 else True).wait_recv()
                k = lax.rem(chip + (CHIPS - t if side == 0 else t), CHIPS)
                rs[side, i, t - 2] = add_bf16(rs[side, i, t - 2], own[i, pl.ds(pl.multiple_of(k * share, share), share)])
                rs_copy(side, i, t, False).start()

    def rs_final(i):
        mine = lambda: own[i, pl.ds(pl.multiple_of(chip * share, share), share)]

        @pl.when(chip >= 1)
        def _():
            rs_copy(0, i, last, True).wait_recv()

        @pl.when(chip < last)
        def _():
            rs_copy(1, i, last, True).wait_recv()

        @pl.when(chip == 0)
        def _():
            mid[i] = add_bf16(mid[i], add_bf16(mine(), rs[1, i, last - 1]))

        @pl.when(chip == last)
        def _():
            mid[i] = add_bf16(mid[i], add_bf16(mine(), rs[0, i, last - 1]))

        @pl.when((chip >= 1) & (chip < last))
        def _():
            mid[i] = add_bf16(mid[i], add_bf16(mine(), rs[0, i, last - 1], rs[1, i, last - 1]))

    def ag_copy(g, side, hop):
        origin = chip - hop if side == 0 else chip + hop
        slot = out_any.at[core, pl.ds(2 * g, 2), origin]
        src = mid.at[pl.ds(2 * g, 2)] if hop == 0 else slot
        return remote(src, slot, ag_s.at[g, side, hop], ag_r.at[g, origin], tp=me + 2 if side == 0 else me - 2)

    def agp_copy(g, origin, fresh=False, incoming=False):
        slot = out_any.at[1 - core if incoming else core, pl.ds(2 * g, 2), origin]
        return remote(mid.at[pl.ds(2 * g, 2)] if fresh else slot, slot, agp_s.at[g, origin], agp_r.at[g, origin], tp=partner)

    def put_copy(g):
        return pltpu.make_async_copy(mid.at[pl.ds(2 * g, 2)], out_any.at[core, pl.ds(2 * g, 2), chip], put_sem.at[g])

    def ag_first(g):
        put_copy(g).start()

        @pl.when(chip < last)
        def _():
            ag_copy(g, 0, 0).start()

        @pl.when(chip > 0)
        def _():
            ag_copy(g, 1, 0).start()

        agp_copy(g, chip, fresh=True).start()

    def ag_step(g, d):
        for side, origin, valid, onward in sides(d):
            @pl.when(valid)
            def _():
                slot = out_any.at[core, pl.ds(2 * g, 2), origin]
                remote(slot, slot, ag_s.at[g, side, d - 1], ag_r.at[g, origin], tp=partner).wait_recv()
                if d < last:
                    @pl.when(onward)
                    def _():
                        ag_copy(g, side, d).start()
                agp_copy(g, origin).start()

    def x_copy(n):
        seq = core + (1 - 2 * core) * (1 - lax.rem(n, 2))
        return pltpu.make_async_copy(x_any.at[seq, lax.div(n, 2)], x_buf.at[lax.rem(n, 2)], x_sem.at[lax.rem(n, 2)])

    def met_copy(i):
        return remote(part, met.at[lax.rem(i, 2)], met_s, met_r.at[lax.rem(i, 2)], tp=partner)

    barrier = pltpu.get_barrier_semaphore()
    for where in ({'tp': partner}, {'dp': across_x}, {'dp': across_y}):
        pl.semaphore_signal(barrier, inc=1, device_id=where, device_id_type=MESH)

    @pl.when(chip < last)
    def _():
        pl.semaphore_signal(barrier, inc=1, device_id={'tp': me + 2}, device_id_type=MESH)

    @pl.when(chip > 0)
    def _():
        pl.semaphore_signal(barrier, inc=1, device_id={'tp': me - 2}, device_id_type=MESH)

    loads = [pltpu.make_async_copy(a, b, load_sem.at[k]) for k, (a, b) in enumerate(((wq_any, wq), (wk_any, wk), (wv_any, wv), (wg_any, wg), (wo_any, wo)))]
    x_copy(0).start()
    for load in loads:
        load.start()
    mid_load = pltpu.make_async_copy(x_any.at[core, :, chip], mid, mid_sem)
    mid_load.start()
    pl.semaphore_wait(barrier, 3 + (chip < last).astype(jnp.int32) + (chip > 0).astype(jnp.int32))

    for p in range(2):
        @pl.when(chip < last)
        def _():
            z_copy(0, 0, p).start()

        @pl.when(chip > 0)
        def _():
            z_copy(1, 0, p).start()

        partner_copy(chip, p, own_shard=True).start()

    state_ref[...] = state_in[...]
    for load in loads:
        load.wait()

    def attend(n, carry):
        i, k = lax.div(n, 2), lax.rem(n, 2)
        seq = core + (1 - 2 * core) * (1 - k)
        x_copy(n).wait()

        @pl.when(n < 2 * BLOCKS - 1)
        def _():
            x_copy(n + 1).start()

        h = normalize(x_buf[k].reshape(rows, part.shape[1]).astype(F32), gain1[...], bias1[...]).astype(BF16)
        q_raw = jnp.dot(h, wq[...], preferred_element_type=F32)
        k_raw = jnp.dot(h, wk[...], preferred_element_type=F32)
        v_all = jnp.dot(h, wv[...], preferred_element_type=F32).astype(BF16)
        g_all = jnp.dot(h, wg[...], preferred_element_type=F32)
        cos_lo, sin_lo = table[0], table[1]
        mixed = []
        subs = rows // chunk
        for sub in range(subs):
            span = slice(sub * chunk, (sub + 1) * chunk)
            cos_hi, sin_hi = base[seq, i * subs + sub, 0:1, :], base[seq, i * subs + sub, 1:2, :]
            cos_t = cos_hi * cos_lo - sin_hi * sin_lo
            sin_t = sin_hi * cos_lo + cos_hi * sin_lo

            def rotate(raw):
                first, second = raw[span, :half], raw[span, half:]
                return jnp.concatenate([first * cos_t - second * sin_t, second * cos_t + first * sin_t], axis=-1)

            queries = rotate(q_raw).astype(BF16)
            keys = (rotate(k_raw) * key_dim ** -0.5).astype(BF16)
            values = v_all[span]
            state = state_ref[seq, 0]
            scores = lax.dot_general(queries, keys, (((1,), (1,)), ((), ())), preferred_element_type=F32) * decay[...]
            retained = jnp.dot(scores.astype(BF16), values, preferred_element_type=F32)
            retained += jnp.dot(queries, state.astype(BF16), preferred_element_type=F32) * edge[:, 0:1]
            keys_decayed = (keys.astype(F32) * edge[:, 1:2]).astype(BF16)
            grown = lax.dot_general(keys_decayed, values, (((0,), (0,)), ((), ())), preferred_element_type=F32)
            state_ref[seq, 0] = state * edge[0:1, 2:3] + grown
            row_mean = jnp.mean(retained, axis=-1, keepdims=True)
            centered = retained - row_mean
            variance = jnp.mean(centered * centered, axis=-1, keepdims=True)
            normed = centered * lax.rsqrt(variance + GROUP_EPS)
            mixed.append((jax.nn.silu(g_all[span]) * normed).astype(BF16))
        u = jnp.dot(jnp.concatenate(mixed, axis=0), wo[...], preferred_element_type=F32).astype(BF16)

        @pl.when(k == 1)
        def _():
            met_copy(i).wait_send()

        part[...] = u

        @pl.when(k == 0)
        def _():
            @pl.when(i >= 2)
            def _():
                pl.semaphore_wait(credit, 1)

            met_copy(i).start()

        @pl.when(k == 1)
        def _():
            met_copy(i).wait_recv()
            own[i] = add_bf16(part[...], met[lax.rem(i, 2)])

            @pl.when(i < BLOCKS - 2)
            def _():
                pl.semaphore_signal(credit, inc=1, device_id={'tp': partner}, device_id_type=MESH)

            rs_first(i)

            @pl.when(i >= 1)
            def _():
                rs_step(i - 1, 2)

            @pl.when(i >= 2)
            def _():
                rs_step(i - 2, 3)

        @pl.when(n == 2)
        def _():
            spread_first(1)

        @pl.when(n == 4)
        def _():
            spread_first(2)
            spread_second(1)

        @pl.when(n == 6)
        def _():
            spread_second(2)
            spread_third(1)

        @pl.when(n == 7)
        def _():
            spread_first(3)

        return carry

    lax.fori_loop(0, 2 * BLOCKS, attend, 0)

    mid_load.wait()

    def shard_of(e, other):
        origin = chip if e == 0 else chip + 1 - 2 * lax.rem(chip, 2) if e == 1 else 2 - lax.div(chip, 2) if e == 2 else 3 - 3 * lax.div(chip, 2)
        return origin, 2 * origin + (1 - core if other else core)

    slots = ((wv, wo), (wg, wd))

    def tile_copies(step):
        e, other = step // 2, step % 2
        shard = shard_of(e, other)[1]
        sources = (up_any, down_any) if step == 0 else (up_all.at[shard], down_all.at[shard])
        return [pltpu.make_async_copy(sources[p], slots[step % 2][p], tile_sem.at[step % 2, p]) for p in range(2)]

    def arrive(step):
        e, other = step // 2, step % 2
        if other:
            for p in range(2):
                partner_copy(shard_of(e, 0)[0], p, incoming=True).wait_recv()
        elif e > 0:
            spread_third(e) if e > 1 else None

    def feed_forward(g):
        width = mid.shape[2]
        for copy in tile_copies(0):
            copy.start()
        x_mid = mid[pl.ds(2 * g, 2)].reshape(2 * share, width).astype(F32)
        hid[...] = normalize(x_mid, gain2[...], bias2[...]).astype(BF16)
        for step in range(2 * CHIPS):
            if step + 1 < 2 * CHIPS:
                if g == 0:
                    arrive(step + 1)
                for copy in tile_copies(step + 1):
                    copy.start()
            for copy in tile_copies(step):
                copy.wait()
            up, down = slots[step % 2]
            pre = jnp.dot(hid[...], up[...], preferred_element_type=F32)
            act = (0.5 * pre * (1.0 + lax.erf(pre * 0.5 ** 0.5))).astype(BF16)
            grown = jnp.dot(act, down[...], preferred_element_type=F32)
            acc[...] = grown if step == 0 else acc[...] + grown
        f = acc[...].astype(BF16).astype(F32)
        x_mid = mid[pl.ds(2 * g, 2)].reshape(2 * share, width).astype(F32)
        mid[pl.ds(2 * g, 2)] = (x_mid + f).astype(BF16).reshape(2, share, width)

    rs_final(0)
    rs_final(1)
    spread_second(3)
    feed_forward(0)
    ag_first(0)
    rs_step(2, 3)
    rs_step(3, 2)
    rs_step(3, 3)
    rs_final(2)
    rs_final(3)
    ag_step(0, 1)
    feed_forward(1)
    ag_first(1)
    for d in range(1, CHIPS):
        if d > 1:
            ag_step(0, d)
        ag_step(1, d) if d < 2 else None
    ag_step(1, 2)
    ag_step(1, 3)

    for g in range(2):
        put_copy(g).wait()
        for origin in range(CHIPS):
            agp_copy(g, origin).wait_send()
            agp_copy(g, origin, incoming=True).wait_recv()
        for hop in range(last):
            @pl.when((chip >= hop) & (chip < last))
            def _():
                ag_copy(g, 0, hop).wait_send()

            @pl.when((chip + hop <= last) & (chip > 0))
            def _():
                ag_copy(g, 1, hop).wait_send()
    for p in range(2):
        partner_copy(chip, p, own_shard=True).wait_send()
        for hop in range(last):
            @pl.when((chip >= hop) & (chip < last))
            def _():
                z_copy(0, hop, p).wait_send()

            @pl.when((chip + hop <= last) & (chip > 0))
            def _():
                z_copy(1, hop, p).wait_send()
        for d in range(1, CHIPS):
            for side, origin, valid, onward in sides(d):
                @pl.when(valid)
                def _():
                    partner_copy(origin, p).wait_send()
                    second_copy(origin, p).wait_send()
                    for axis in range(2):
                        first_copy(axis, origin, p).wait_send()

    def settle(i, carry):
        for side, end in ((0, 0), (1, last)):
            for t in range(1, CHIPS):
                @pl.when((chip == end) | (rs_senders(side, t) if t > 1 else chip < 0))
                def _():
                    rs_copy(side, i, t, True).wait_send()
        return carry

    lax.fori_loop(0, BLOCKS, settle, 0)


def solution(mesh):
    members = mesh.shape['tp']

    def local_layer(x_in, start_pos, kv_state, ln1_gain, ln1_bias, w_q, w_k, w_v, w_g, w_o, ln2_gain, ln2_bias, w_up, w_down):
        seqs, chunk_len, d_model = x_in.shape
        key_dim = kv_state.shape[2]
        half = key_dim // 2
        rows = chunk_len // BLOCKS
        share = rows // CHIPS
        chunk = min(CHUNK, rows)
        me = lax.axis_index('tp')
        log_gamma = jnp.log1p(-jnp.exp2(-5.0 - me.astype(F32)))
        ids = jnp.arange(chunk)
        gap = ids[:, None] - ids[None, :]
        decay = jnp.where(gap >= 0, jnp.exp(jnp.maximum(gap, 0).astype(F32) * log_gamma), 0.0)
        lane = jnp.arange(128)[None, :]
        power = jnp.where(lane == 0, ids[:, None] + 1, jnp.where(lane == 1, chunk - 1 - ids[:, None], chunk))
        edge = jnp.exp(power.astype(F32) * log_gamma)
        inv_freq = jnp.power(ROPE_BASE, -jnp.arange(half).astype(F32) / half)
        low = ids.astype(F32)[:, None] * inv_freq[None, :]
        table = jnp.stack([jnp.cos(low), jnp.sin(low)])
        high = (start_pos[:, None] + jnp.arange(chunk_len // chunk)[None, :] * chunk).astype(F32)[:, :, None] * inv_freq
        base = jnp.stack([jnp.cos(high), jnp.sin(high)], axis=2)

        anywhere = pl.BlockSpec(memory_space=pl.ANY)
        vmem = pl.BlockSpec(memory_space=pltpu.VMEM)
        dma = lambda *shape: pltpu.SemaphoreType.DMA(shape)
        out, state, _, _ = pl.pallas_call(
            layer_kernel,
            in_specs=[anywhere, vmem, vmem, vmem, vmem, vmem] + [anywhere] * 7 + [vmem] * 4,
            out_specs=[anywhere, vmem, anywhere, anywhere],
            out_shape=[
                jax.ShapeDtypeStruct((seqs, BLOCKS, CHIPS, share, d_model), BF16),
                jax.ShapeDtypeStruct(kv_state.shape, F32),
                jax.ShapeDtypeStruct((members,) + w_up.shape, BF16),
                jax.ShapeDtypeStruct((members,) + w_down.shape, BF16),
            ],
            scratch_shapes=[
                pltpu.VMEM(w_q.shape, BF16), pltpu.VMEM(w_k.shape, BF16), pltpu.VMEM(w_v.shape, BF16), pltpu.VMEM(w_g.shape, BF16),
                pltpu.VMEM(w_o.shape, BF16), pltpu.VMEM(w_down.shape, BF16),
                pltpu.VMEM((2, CHIPS, share, d_model), BF16), pltpu.VMEM((rows, d_model), BF16), pltpu.VMEM((2, rows, d_model), BF16),
                pltpu.VMEM((BLOCKS, rows, d_model), BF16), pltpu.VMEM((2, BLOCKS, CHIPS - 1, share, d_model), BF16),
                pltpu.VMEM((BLOCKS, share, d_model), BF16), pltpu.VMEM((2 * share, d_model), BF16), pltpu.VMEM((2 * share, d_model), F32),
                dma(5), dma(2), pltpu.SemaphoreType.DMA, dma(2, 2), pltpu.SemaphoreType.DMA, dma(2), pltpu.SemaphoreType.REGULAR,
                dma(2, BLOCKS, 3), dma(2, BLOCKS, 3), dma(2, 3, 2), dma(4, 2), dma(2, 4, 2), dma(2, 4, 2), dma(4, 2), dma(4, 2), dma(4, 2), dma(4, 2),
                dma(2, 2, 3), dma(2, 4), dma(2, 4), dma(2, 4), dma(2),
            ],
            compiler_params=pltpu.CompilerParams(collective_id=0, has_side_effects=True, vmem_limit_bytes=67043328),
            name="layer",
        )(x_in.reshape(seqs, BLOCKS, CHIPS, share, d_model), kv_state, *(a[None, :] for a in (ln1_gain, ln1_bias, ln2_gain, ln2_bias)), w_q, w_k, w_v, w_g, w_o, w_up, w_down, base, table, decay, edge)
        return out.reshape(seqs, chunk_len, d_model), state

    in_specs = (P('dp', None, None), P('dp'), P('dp', 'tp', None, None), P(), P(), P(None, 'tp'), P(None, 'tp'), P(None, 'tp'), P(None, 'tp'), P('tp', None), P(), P(), P(None, 'tp'), P('tp', None))
    out_specs = (P('dp', None, None), P('dp', 'tp', None, None))
    return jax.shard_map(local_layer, mesh=mesh, in_specs=in_specs, out_specs=out_specs, check_vma=False)
```

time: 903 us -> 368 us (0.41)
  waiting for transfers between devices: 661 us -> 0 us
  Pallas kernels: 0 us -> 348 us
  matrix products: 146 us -> 0 us
  other arithmetic: 73.3 us -> 4.48 us
  between operations: 14.9 us -> 0.78 us
  local copies, waits for them, and re-layouts: 4.91 us -> 15.2 us
    psum x2 -> x0, waiting for transfers between devices: 661 us -> none  [the longest x1 335 us: local_layer(): attn_out = lax.psum(attn_part, 'tp')]
    pallas_call x0 -> x1, Pallas kernels: none -> 348 us  [local_layer(): pl.pallas_call(layer_kernel, in_specs=[anywhere, vmem, vmem, vmem, vmem,...]
    dot_general x10 -> x0, matrix products: 146 us -> none  [the longest x1 31.1 us: feed_forward(): jnp.einsum('bcf,fd->bcd', activated, w_down, preferred_element_type=jnp.f...]
    reduce_sum x5 -> x0, other arithmetic: 32 us -> none  [the longest x2 16.8 us: layer_norm(): row_mean = jnp.mean(x_f32, axis=-1, keepdims=True)]
    convert_element_type x2, other arithmetic: 20 us -> 0.73 us  [the longest x1 0.73 us: local_layer(): (start_pos[:, None] + jnp.arange(chunk_len // chunk)[None, :] * chunk).as...]
    select_n x1, other arithmetic: 11.3 us -> 0.76 us  [local_layer(): jnp.where(gap >= 0, jnp.exp(jnp.maximum(gap, 0).astype(F32) * log_gamma),...]
    unnamed x34 -> x4, local copies, waits for them, and re-layouts: 4.91 us -> 15.2 us
    concatenate x1 -> x0, other arithmetic: 9.93 us -> none  [rotate_half(): jnp.concatenate([first_half * cos_t - second_half * sin_t, second_half *...]
  transfers between devices with their start and end apart: 2 -> 0, of which waited for: 2 -> 0; matrix products, arithmetic and copies ran while one was open for 1% -> 0% of each run, Pallas kernels for 0% -> 0%
where the time goes in v1:
time: 368 us
  Pallas kernels  348 us (95%)
  local copies, waits for them, and re-layouts  15.2 us (4%)
  other arithmetic  4.48 us (1%)
    pallas_call x1, Pallas kernels, local_layer(): pl.pallas_call(layer_kernel, in_specs=[anywhere, vmem, vmem, vmem, vmem,...  348 us
    unnamed x4, local copies, waits for them, and re-layouts  15.2 us

profile of v1, /device:TPU:0, one launch (start us, length us, event | category | flops | bytes accessed | tf_op | source)
XLA Modules:
  0.0 368.0 jit_solution(17984225093756853620)
XLA Ops:
  0.7 0.7 add_convert_fusion
  1.5 0.3 multiply_cosine_fusion.1
  1.8 0.6 pad_maximum_fusion.1.base
  2.4 0.8 multiply_exponential_fusion.edge
  3.2 0.5 multiply_cosine_fusion
  3.8 0.7 pad_maximum_fusion.table
  4.5 0.8 exponential_select_fusion.decay
  5.2 347.5 %layer.1 = (bf16[2,4,4,128,2048]{4,3,2,1,0:T(8,128)(2,1)}, f32[2,1,256,512]{3,2,1,0:T(8,128)}, bf16[8,2048,512]{2,1,0:T(8,128)(2,1)}, bf16[8,512,2048]{2,1,0:T(8,128)(2,1)}) custom-call(bf16[2,4,4,128,2048]{4,3,2,1,0:T(8,128)(2,1)} %bitcast.7, f32[2,1,256,512]{3,2,1,0:T(8,128)} %state_in.1, f32[1,2048]{1,0:T(1,128)} %bitcast.10, f32[1,2048]{1,0:T(1,128)} %bitcast.11, ...), custom_call_target="tpu_custom_call" | custom-call | tf_op jit(solution)/shard_map/layer/pallas_call | solution.py:469
  352.8 0.0 copy-start
  352.8 14.2 %copy.19 = bf16[2,2048,2048]{2,1,0:T(8,128)(2,1)} copy(bf16[2,2048,2048]{2,1,0:T(8,128)(2,1)} %bitcast.8) | data formatting | bytes 33554432
  367.0 0.0 copy-done
  367.1 1.0 copy.20
  (6 shorter events, 0.0 us)
Async XLA Ops:
  352.8 14.3 %copy-start = (f32[2,1,256,512]{3,2,1,0:T(8,128)S(1)}, f32[2,1,256,512]{3,2,1,0:T(8,128)}, u32[]{:S(2)}) copy-start(f32[2,1,256,512]{3,2,1,0:T(8,128)} %get-tuple-element.17) | copy-start | bytes 3145732

commit v2 on v1

v2 whole, which is shorter than its diff:
```python
import jax
import jax.numpy as jnp
from jax import lax
from jax.experimental import pallas as pl
from jax.experimental.pallas import tpu as pltpu
from jax.sharding import PartitionSpec as P

NORM_EPS = 1e-5
GROUP_EPS = 1e-6
ROPE_BASE = 10000.0
CHUNK = 256
BLOCKS = 4
CHIPS = 4
F32 = jnp.float32
BF16 = jnp.bfloat16
MESH = pl.DeviceIdType.MESH
GROUPS = ((0, 1), (2,), (3,))
LOOP = {
    0: (
        ('s1', 'm', 'f1', 0), ('s1', 'm', 'n1', 1), ('s1', 'm', 'f1', 1),
    ),
    1: (
        ('s1', 'm', 'n1', 0),
    ),
    2: (
        ('s1', 'e', 1, 0),
    ),
    3: (
        ('s1', 'e', 1, 1), ('s1', 'e', 2, 0), ('s2', 'e', 1, 1), ('s1', 'm', 'f2', 0), ('rs', 'm', 0, 2, 'n'), ('s2', 'e', 1, 0),
        ('rs', 'm', 0, 3, 'n'), ('s1', 'e', 3, 0), ('s1', 'm', 'f2', 1), ('s2', 'm', 'f1', 1), ('s3', 'e', 1, 0), ('s3', 'e', 1, 1),
    ),
    5: (
        ('rs', 'm', 1, 2, 'n'),
    ),
    6: (
        ('s2', 'm', 'n1', 1), ('s2', 'm', 'n1', 0), ('fin', 'm', 0), ('s1', 'e', 3, 1),
    ),
}
TAIL = (
    ('rs', 'm', 1, 3, 'n'), ('s1', 'e', 2, 1), ('s2', 'm', 'f1', 0), ('rs', 'm', 1, 3, 'f'), ('rs', 'm', 0, 3, 'f'), ('fin', 'e', 1),
    ('s3', 'm', 'f1', 1), ('s3', 'm', 'n1', 0), ('s2', 'm', 'f2', 1), ('s2', 'e', 2, 0), ('s2', 'm', 'f2', 0), ('fin', 'm', 1),
    ('rs', 'm', 2, 2, 'n'), ('fin', 'e', 0), ('s3', 'm', 'n1', 1), ('F', 0, 0), ('s2', 'e', 3, 1), ('s3', 'e', 2, 0), ('s3', 'm', 'f1', 0),
    ('F', 0, 1), ('s2', 'e', 3, 0), ('s2', 'e', 2, 1), ('s3', 'e', 3, 0), ('s3', 'e', 2, 1), ('fin', 'e', 2), ('F', 0, 2), ('F', 0, 3),
    ('rs', 'm', 2, 3, 'n'), ('s3', 'm', 'f2', 0), ('s3', 'm', 'f2', 1), ('rs', 'm', 2, 3, 'f'), ('s3', 'e', 3, 1), ('F', 0, 4),
    ('ag', 'e', 1, 0), ('F', 0, 5), ('F', 0, 6), ('F', 0, 7), ('agf', 0), ('fin', 'm', 2), ('F', 1, 0), ('F', 1, 1), ('F', 1, 2),
    ('rs', 'm', 3, 2, 'n'), ('F', 1, 3), ('F', 1, 4), ('rs', 'm', 3, 3, 'n'), ('F', 1, 5), ('ag', 'm', 'f1', 0), ('ag', 'e', 1, 2),
    ('F', 1, 6), ('ag', 'm', 'f1', 1), ('F', 1, 7), ('rs', 'm', 3, 3, 'f'), ('ag', 'm', 'n1', 0), ('agf', 1), ('fin', 'e', 3),
    ('fin', 'm', 3), ('ag', 'e', 1, 1), ('F', 2, 0), ('F', 2, 1), ('F', 2, 2), ('F', 2, 3), ('F', 2, 4), ('F', 2, 5), ('F', 2, 6),
    ('ag', 'e', 2, 1), ('F', 2, 7), ('ag', 'm', 'f2', 0), ('agf', 2), ('ag', 'm', 'n1', 1), ('ag', 'e', 3, 0), ('ag', 'e', 2, 3),
    ('ag', 'e', 3, 1), ('ag', 'e', 3, 2), ('ag', 'm', 'n1', 2), ('ag', 'm', 'f1', 3), ('ag', 'm', 'f1', 2), ('ag', 'e', 2, 2),
    ('ag', 'm', 'n1', 3), ('ag', 'm', 'f2', 2), ('ag', 'e', 1, 3), ('ag', 'e', 2, 0), ('ag', 'm', 'f2', 1), ('ag', 'm', 'f2', 3),
    ('ag', 'e', 3, 3),
)


def normalize(x_f32, gain, bias):
    row_mean = jnp.mean(x_f32, axis=-1, keepdims=True)
    centered = x_f32 - row_mean
    variance = jnp.mean(centered * centered, axis=-1, keepdims=True)
    return centered * lax.rsqrt(variance + NORM_EPS) * gain + bias


def add_bf16(*terms):
    return sum(t.astype(F32) for t in terms).astype(BF16)


def layer_kernel(x_any, state_in, gain1, bias1, gain2, bias2, wq_any, wk_any, wv_any, wg_any, wo_any, up_any, down_any, base, table, decay, edge,
                 out_any, state_ref, up_all, down_all,
                 wq, wk, wv, wg, wo, wd, x_buf, part, met, own, rs, mid, hid, acc,
                 load_sem, x_sem, mid_sem, tile_sem, met_s, met_r, credit, rs_s, rs_r, z_s, z_r, f_s, f_r, g_s, g_r, p_s, p_r, ag_s, ag_r, agp_s, agp_r, put_sem):
    group, me = lax.axis_index('dp'), lax.axis_index('tp')
    chip, core = lax.div(me, 2), lax.rem(me, 2)
    partner = me + 1 - 2 * core
    across_x = lax.rem(group + 2, 4)
    across_y = group + 1 - 2 * lax.rem(group, 2)
    chunk = decay.shape[0]
    rows, share = own.shape[1], mid.shape[1]
    key_dim, half = wq.shape[1], wq.shape[1] // 2
    last = CHIPS - 1
    far = 1 - 2 * lax.div(chip, 2)
    is_end = (chip == 0) | (chip == last)
    is_middle = (chip > 0) & (chip < last)

    def remote(src, dst, s, r, **where):
        return pltpu.make_async_remote_copy(src_ref=src, dst_ref=dst, send_sem=s, recv_sem=r, device_id=where, device_id_type=MESH)

    def side_of(flow):
        return lax.div(1 - flow, 2)

    weight_all, weight_own = (up_all, down_all), (up_any, down_any)
    quarter = tuple(w.shape[0] // 4 for w in weight_own)

    def origin_of(which):
        return {'n1': chip - far, 'f1': chip + far, 'f2': chip + 2 * far}[which] if isinstance(which, str) else chip + which * far

    def piece(p, shard, q):
        return weight_all[p].at[shard, pl.ds(q * quarter[p], quarter[p])]

    def z_copy(flow, origin, p, own_piece=False):
        slot = piece(p, 2 * origin + core, group)
        src = weight_own[p].at[pl.ds(group * quarter[p], quarter[p])] if own_piece else slot
        return remote(src, slot, z_s.at[side_of(flow), origin, p], z_r.at[origin, p], tp=me + 2 * flow)

    def first_copy(axis, origin, p, q=None):
        slot = piece(p, 2 * origin + core, group if q is None else q)
        return remote(slot, slot, f_s.at[axis, origin, p], f_r.at[axis, origin, p], dp=across_x if axis == 0 else across_y)

    def second_copy(origin, p, q=None):
        slot = piece(p, 2 * origin + core, (across_x if p == 0 else across_y) if q is None else q)
        return remote(slot, slot, g_s.at[origin, p], g_r.at[origin, p], dp=across_y if p == 0 else across_x)

    def partner_copy(origin, p, own_shard=False, incoming=False):
        slot = weight_all[p].at[2 * origin + (1 - core if incoming else core)]
        return remote(weight_own[p] if own_shard else slot, slot, p_s.at[origin, p], p_r.at[origin, p], tp=partner)

    def spread_first(which, p):
        origin = origin_of(which)
        z_copy(far, origin, p).wait_recv()
        if isinstance(which, str):
            z_copy(far if which == 'n1' else -far, origin, p).start()
        for axis in range(2):
            first_copy(axis, origin, p).start()

    def spread_second(which, p):
        origin = origin_of(which)
        first_copy(p, origin, p, across_x if p == 0 else across_y).wait_recv()
        second_copy(origin, p).start()

    def spread_third(which, p):
        origin = origin_of(which)
        first_copy(1 - p, origin, p, across_y if p == 0 else across_x).wait_recv()
        second_copy(origin, p, 3 - group).wait_recv()
        partner_copy(origin, p).start()

    def rs_shard(flow, t):
        return lax.rem(chip - flow * t + CHIPS, CHIPS)

    def rs_copy(flow, i, t, fresh=False):
        side = side_of(flow)
        src = own.at[i, pl.ds(rs_shard(flow, t) * share, share)] if fresh else rs.at[side, i, t - 2]
        return remote(src, rs.at[side, i, t - 1], rs_s.at[side, i, t - 1], rs_r.at[side, i, t - 1], tp=me + 2 * flow)

    def rs_first(i):
        @pl.when(is_end)
        def _():
            for t in range(1, CHIPS):
                rs_copy(far, i, t, fresh=True).start()

    def mine(i, k):
        return own[i, pl.ds(pl.multiple_of(k * share, share), share)]

    def rs_step(i, t, which):
        flow = far if which == 'n' else -far
        side = side_of(flow)
        rs_copy(flow, i, t - 1, fresh=True).wait_recv()
        rs[side, i, t - 2] = add_bf16(rs[side, i, t - 2], mine(i, rs_shard(flow, t)))
        rs_copy(flow, i, t).start()

    def rs_final(kind, i):
        rs_copy(-far, i, last, fresh=True).wait_recv()
        terms = [mine(i, chip), rs[side_of(-far), i, last - 1]]
        if kind == 'm':
            rs_copy(far, i, last, fresh=True).wait_recv()
            terms.append(rs[side_of(far), i, last - 1])
        mid[i] = add_bf16(mid[i], add_bf16(*terms))

    def ag_copy(b, flow, origin, fresh=False):
        slot = out_any.at[core, b, origin]
        return remote(mid.at[b] if fresh else slot, slot, ag_s.at[b, side_of(flow), origin], ag_r.at[b, origin], tp=me + 2 * flow)

    def agp_copy(b, origin, fresh=False, incoming=False):
        slot = out_any.at[1 - core if incoming else core, b, origin]
        return remote(mid.at[b] if fresh else slot, slot, agp_s.at[b, origin], agp_r.at[b, origin], tp=partner)

    def put_copy(b):
        return pltpu.make_async_copy(mid.at[b], out_any.at[core, b, chip], put_sem.at[b])

    def ag_first(g):
        for b in GROUPS[g]:
            ag_copy(b, far, chip, fresh=True).start()

            @pl.when(is_middle)
            def _():
                ag_copy(b, -far, chip, fresh=True).start()

            agp_copy(b, chip, fresh=True).start()
            put_copy(b).start()

    def ag_step(which, b):
        origin = origin_of(which)
        ag_copy(b, far, origin).wait_recv()
        if isinstance(which, str):
            ag_copy(b, far if which == 'n1' else -far, origin).start()
        agp_copy(b, origin).start()

    def serve(item):
        kind, where, args = item[0], item[1], item[2:]

        @pl.when(is_end if where == 'e' else is_middle)
        def _():
            if kind == 's1':
                spread_first(*args)
            elif kind == 's2':
                spread_second(*args)
            elif kind == 's3':
                spread_third(*args)
            elif kind == 'rs':
                rs_step(*args)
            elif kind == 'fin':
                rs_final(where, *args)
            else:
                ag_step(*args)

    def x_copy(n):
        seq = core + (1 - 2 * core) * (1 - lax.rem(n, 2))
        return pltpu.make_async_copy(x_any.at[seq, lax.div(n, 2)], x_buf.at[lax.rem(n, 2)], x_sem.at[lax.rem(n, 2)])

    def met_copy(i):
        return remote(part, met.at[lax.rem(i, 2)], met_s, met_r.at[lax.rem(i, 2)], tp=partner)

    barrier = pltpu.get_barrier_semaphore()
    for where in ({'tp': partner}, {'dp': across_x}, {'dp': across_y}):
        pl.semaphore_signal(barrier, inc=1, device_id=where, device_id_type=MESH)

    @pl.when(chip < last)
    def _():
        pl.semaphore_signal(barrier, inc=1, device_id={'tp': me + 2}, device_id_type=MESH)

    @pl.when(chip > 0)
    def _():
        pl.semaphore_signal(barrier, inc=1, device_id={'tp': me - 2}, device_id_type=MESH)

    loads = [pltpu.make_async_copy(a, b, load_sem.at[k]) for k, (a, b) in enumerate(((wq_any, wq), (wk_any, wk), (wv_any, wv), (wg_any, wg), (wo_any, wo)))]
    x_copy(0).start()
    for load in loads:
        load.start()
    mid_load = pltpu.make_async_copy(x_any.at[core, :, chip], mid, mid_sem)
    mid_load.start()
    pl.semaphore_wait(barrier, 4 + is_middle.astype(jnp.int32))

    for p in range(2):
        z_copy(far, chip, p, own_piece=True).start()

        @pl.when(is_middle)
        def _():
            z_copy(-far, chip, p, own_piece=True).start()

        partner_copy(chip, p, own_shard=True).start()

    state_ref[...] = state_in[...]
    for load in loads:
        load.wait()
    mid_load.wait()

    def attend(n, carry):
        i, k = lax.div(n, 2), lax.rem(n, 2)
        seq = core + (1 - 2 * core) * (1 - k)
        x_copy(n).wait()

        @pl.when(n < 2 * BLOCKS - 1)
        def _():
            x_copy(n + 1).start()

        h = normalize(x_buf[k].reshape(rows, part.shape[1]).astype(F32), gain1[...], bias1[...]).astype(BF16)
        q_raw = jnp.dot(h, wq[...], preferred_element_type=F32)
        k_raw = jnp.dot(h, wk[...], preferred_element_type=F32)
        v_all = jnp.dot(h, wv[...], preferred_element_type=F32).astype(BF16)
        g_all = jnp.dot(h, wg[...], preferred_element_type=F32)
        cos_lo, sin_lo = table[0], table[1]
        mixed = []
        subs = rows // chunk
        for sub in range(subs):
            span = slice(sub * chunk, (sub + 1) * chunk)
            cos_hi, sin_hi = base[seq, i * subs + sub, 0:1, :], base[seq, i * subs + sub, 1:2, :]
            cos_t = cos_hi * cos_lo - sin_hi * sin_lo
            sin_t = sin_hi * cos_lo + cos_hi * sin_lo

            def rotate(raw):
                first, second = raw[span, :half], raw[span, half:]
                return jnp.concatenate([first * cos_t - second * sin_t, second * cos_t + first * sin_t], axis=-1)

            queries = rotate(q_raw).astype(BF16)
            keys = (rotate(k_raw) * key_dim ** -0.5).astype(BF16)
            values = v_all[span]
            state = state_ref[seq, 0]
            scores = lax.dot_general(queries, keys, (((1,), (1,)), ((), ())), preferred_element_type=F32) * decay[...]
            retained = jnp.dot(scores.astype(BF16), values, preferred_element_type=F32)
            retained += jnp.dot(queries, state.astype(BF16), preferred_element_type=F32) * edge[:, 0:1]
            keys_decayed = (keys.astype(F32) * edge[:, 1:2]).astype(BF16)
            grown = lax.dot_general(keys_decayed, values, (((0,), (0,)), ((), ())), preferred_element_type=F32)
            state_ref[seq, 0] = state * edge[0:1, 2:3] + grown
            row_mean = jnp.mean(retained, axis=-1, keepdims=True)
            centered = retained - row_mean
            variance = jnp.mean(centered * centered, axis=-1, keepdims=True)
            normed = centered * lax.rsqrt(variance + GROUP_EPS)
            mixed.append((jax.nn.silu(g_all[span]) * normed).astype(BF16))
        u = jnp.dot(jnp.concatenate(mixed, axis=0), wo[...], preferred_element_type=F32).astype(BF16)

        @pl.when(k == 1)
        def _():
            met_copy(i).wait_send()

        part[...] = u

        @pl.when(k == 0)
        def _():
            @pl.when(i >= 2)
            def _():
                pl.semaphore_wait(credit, 1)

            met_copy(i).start()

        @pl.when(k == 1)
        def _():
            met_copy(i).wait_recv()
            own[i] = add_bf16(part[...], met[lax.rem(i, 2)])

            @pl.when(i < BLOCKS - 2)
            def _():
                pl.semaphore_signal(credit, inc=1, device_id={'tp': partner}, device_id_type=MESH)

            rs_first(i)

        for turn, items in LOOP.items():
            @pl.when(n == turn)
            def _():
                for item in items:
                    serve(item)

        return carry

    lax.fori_loop(0, 2 * BLOCKS, attend, 0)

    def origin_at(e):
        return (chip, chip + 1 - 2 * lax.rem(chip, 2), 2 - lax.div(chip, 2), 3 - 3 * lax.div(chip, 2))[e]

    slots = ((wv, wo), (wg, wd))

    def tile_copies(step):
        shard = 2 * origin_at(step // 2) + (1 - core if step % 2 else core)
        sources = (up_any, down_any) if step == 0 else (up_all.at[shard], down_all.at[shard])
        return [pltpu.make_async_copy(sources[p], slots[step % 2][p], tile_sem.at[step % 2, p]) for p in range(2)]

    def ffn_tile(height, step):
        for copy in tile_copies(step):
            copy.wait()
        up, down = slots[step % 2]
        pre = jnp.dot(hid[:height], up[...], preferred_element_type=F32)
        act = (0.5 * pre * (1.0 + lax.erf(pre * 0.5 ** 0.5))).astype(BF16)
        grown = jnp.dot(act, down[...], preferred_element_type=F32)
        acc[:height] = grown if step == 0 else acc[:height] + grown

    def ffn_step(g, step):
        first, count = GROUPS[g][0], len(GROUPS[g])
        height, width = count * share, mid.shape[2]
        x_mid = lambda: mid[first:first + count].reshape(height, width).astype(F32)
        if g == 0 and step % 2:
            for p in range(2):
                partner_copy(origin_at(step // 2), p, incoming=True).wait_recv()
        for copy in tile_copies(step):
            copy.start()
        if step == 0:
            hid[:height] = normalize(x_mid(), gain2[...], bias2[...]).astype(BF16)
        else:
            ffn_tile(height, step - 1)
        if step == 2 * CHIPS - 1:
            ffn_tile(height, step)
            f = acc[:height].astype(BF16).astype(F32)
            mid[first:first + count] = (x_mid() + f).astype(BF16).reshape(count, share, width)

    for item in TAIL:
        if item[0] == 'F':
            ffn_step(*item[1:])
        elif item[0] == 'agf':
            ag_first(*item[1:])
        else:
            serve(item)

    for b in range(BLOCKS):
        put_copy(b).wait()
        ag_copy(b, far, chip).wait_send()
        for origin in range(CHIPS):
            agp_copy(b, origin).wait_send()
            agp_copy(b, origin, incoming=True).wait_recv()
    for p in range(2):
        z_copy(far, chip, p).wait_send()
        partner_copy(chip, p, own_shard=True).wait_send()

    def settle_weights(which):
        for p in range(2):
            origin = origin_of(which)
            partner_copy(origin, p).wait_send()
            second_copy(origin, p).wait_send()
            for axis in range(2):
                first_copy(axis, origin, p).wait_send()
            if isinstance(which, str):
                z_copy(far if which == 'n1' else -far, origin, p).wait_send()

    @pl.when(is_end)
    def _():
        for which in (1, 2, 3):
            settle_weights(which)
        for i in range(BLOCKS):
            for t in range(1, CHIPS):
                rs_copy(far, i, t, fresh=True).wait_send()

    @pl.when(is_middle)
    def _():
        for which in ('n1', 'f1', 'f2'):
            settle_weights(which)
        for p in range(2):
            z_copy(-far, chip, p).wait_send()
        for i in range(BLOCKS):
            for flow, t in ((far, 2), (far, 3), (-far, 3)):
                rs_copy(flow, i, t).wait_send()
            ag_copy(i, -far, chip).wait_send()
            for which in ('n1', 'f1', 'f2'):
                ag_copy(i, far if which == 'n1' else -far, origin_of(which)).wait_send()


def solution(mesh):
    members = mesh.shape['tp']

    def local_layer(x_in, start_pos, kv_state, ln1_gain, ln1_bias, w_q, w_k, w_v, w_g, w_o, ln2_gain, ln2_bias, w_up, w_down):
        seqs, chunk_len, d_model = x_in.shape
        key_dim = kv_state.shape[2]
        half = key_dim // 2
        rows = chunk_len // BLOCKS
        share = rows // CHIPS
        chunk = min(CHUNK, rows)
        me = lax.axis_index('tp')
        log_gamma = jnp.log1p(-jnp.exp2(-5.0 - me.astype(F32)))
        ids = jnp.arange(chunk)
        gap = ids[:, None] - ids[None, :]
        decay = jnp.where(gap >= 0, jnp.exp(jnp.maximum(gap, 0).astype(F32) * log_gamma), 0.0)
        lane = jnp.arange(128)[None, :]
        power = jnp.where(lane == 0, ids[:, None] + 1, jnp.where(lane == 1, chunk - 1 - ids[:, None], chunk))
        edge = jnp.exp(power.astype(F32) * log_gamma)
        inv_freq = jnp.power(ROPE_BASE, -jnp.arange(half).astype(F32) / half)
        low = ids.astype(F32)[:, None] * inv_freq[None, :]
        table = jnp.stack([jnp.cos(low), jnp.sin(low)])
        high = (start_pos[:, None] + jnp.arange(chunk_len // chunk)[None, :] * chunk).astype(F32)[:, :, None] * inv_freq
        base = jnp.stack([jnp.cos(high), jnp.sin(high)], axis=2)

        anywhere = pl.BlockSpec(memory_space=pl.ANY)
        vmem = pl.BlockSpec(memory_space=pltpu.VMEM)
        dma = lambda *shape: pltpu.SemaphoreType.DMA(shape)
        out, state, _, _ = pl.pallas_call(
            layer_kernel,
            in_specs=[anywhere, vmem, vmem, vmem, vmem, vmem] + [anywhere] * 7 + [vmem] * 4,
            out_specs=[anywhere, vmem, anywhere, anywhere],
            out_shape=[
                jax.ShapeDtypeStruct((seqs, BLOCKS, CHIPS, share, d_model), BF16),
                jax.ShapeDtypeStruct(kv_state.shape, F32),
                jax.ShapeDtypeStruct((members,) + w_up.shape, BF16),
                jax.ShapeDtypeStruct((members,) + w_down.shape, BF16),
            ],
            scratch_shapes=[
                pltpu.VMEM(w_q.shape, BF16), pltpu.VMEM(w_k.shape, BF16), pltpu.VMEM(w_v.shape, BF16), pltpu.VMEM(w_g.shape, BF16),
                pltpu.VMEM(w_o.shape, BF16), pltpu.VMEM(w_down.shape, BF16),
                pltpu.VMEM((2, CHIPS, share, d_model), BF16), pltpu.VMEM((rows, d_model), BF16), pltpu.VMEM((2, rows, d_model), BF16),
                pltpu.VMEM((BLOCKS, rows, d_model), BF16), pltpu.VMEM((2, BLOCKS, CHIPS - 1, share, d_model), BF16),
                pltpu.VMEM((BLOCKS, share, d_model), BF16), pltpu.VMEM((2 * share, d_model), BF16), pltpu.VMEM((2 * share, d_model), F32),
                dma(5), dma(2), pltpu.SemaphoreType.DMA, dma(2, 2), pltpu.SemaphoreType.DMA, dma(2), pltpu.SemaphoreType.REGULAR,
                dma(2, BLOCKS, 3), dma(2, BLOCKS, 3), dma(2, 4, 2), dma(4, 2), dma(2, 4, 2), dma(2, 4, 2), dma(4, 2), dma(4, 2), dma(4, 2), dma(4, 2),
                dma(BLOCKS, 2, 4), dma(BLOCKS, 4), dma(BLOCKS, 4), dma(BLOCKS, 4), dma(BLOCKS),
            ],
            compiler_params=pltpu.CompilerParams(collective_id=0, has_side_effects=True, vmem_limit_bytes=67043328),
            name="layer",
        )(x_in.reshape(seqs, BLOCKS, CHIPS, share, d_model), kv_state, *(a[None, :] for a in (ln1_gain, ln1_bias, ln2_gain, ln2_bias)), w_q, w_k, w_v, w_g, w_o, w_up, w_down, base, table, decay, edge)
        return out.reshape(seqs, chunk_len, d_model), state

    in_specs = (P('dp', None, None), P('dp'), P('dp', 'tp', None, None), P(), P(), P(None, 'tp'), P(None, 'tp'), P(None, 'tp'), P(None, 'tp'), P('tp', None), P(), P(), P(None, 'tp'), P('tp', None))
    out_specs = (P('dp', None, None), P('dp', 'tp', None, None))
    return jax.shard_map(local_layer, mesh=mesh, in_specs=in_specs, out_specs=out_specs, check_vma=False)
```

time: 368 us -> 304 us (0.83)
  Pallas kernels: 348 us -> 283 us
    pallas_call x1, Pallas kernels: 348 us -> 283 us  [local_layer(): pl.pallas_call(layer_kernel, in_specs=[anywhere, vmem, vmem, vmem, vmem,...]
where the time goes in v2:
time: 304 us
  Pallas kernels  283 us (93%)
  local copies, waits for them, and re-layouts  15.2 us (5%)
  other arithmetic  4.48 us (1%)
    pallas_call x1, Pallas kernels, local_layer(): pl.pallas_call(layer_kernel, in_specs=[anywhere, vmem, vmem, vmem, vmem,...  283 us
    unnamed x4, local copies, waits for them, and re-layouts  15.2 us

profile of v2, /device:TPU:0, one launch (start us, length us, event | category | flops | bytes accessed | tf_op | source)
XLA Modules:
  0.0 303.9 jit_solution(8132031617719552252)
XLA Ops:
  0.7 0.7 add_convert_fusion
  1.5 0.3 multiply_cosine_fusion.1
  1.8 0.6 pad_maximum_fusion.1.base
  2.4 0.8 multiply_exponential_fusion.edge
  3.2 0.5 multiply_cosine_fusion
  3.8 0.7 pad_maximum_fusion.table
  4.5 0.8 exponential_select_fusion.decay
  5.2 283.5 %layer.1 = (bf16[2,4,4,128,2048]{4,3,2,1,0:T(8,128)(2,1)}, f32[2,1,256,512]{3,2,1,0:T(8,128)}, bf16[8,2048,512]{2,1,0:T(8,128)(2,1)}, bf16[8,512,2048]{2,1,0:T(8,128)(2,1)}) custom-call(bf16[2,4,4,128,2048]{4,3,2,1,0:T(8,128)(2,1)} %bitcast.7, f32[2,1,256,512]{3,2,1,0:T(8,128)} %state_in.1, f32[1,2048]{1,0:T(1,128)} %bitcast.10, f32[1,2048]{1,0:T(1,128)} %bitcast.11, ...), custom_call_target="tpu_custom_call" | custom-call | tf_op jit(solution)/shard_map/layer/pallas_call | solution.py:448
  288.7 0.0 copy-start
  288.7 14.2 %copy.19 = bf16[2,2048,2048]{2,1,0:T(8,128)(2,1)} copy(bf16[2,2048,2048]{2,1,0:T(8,128)(2,1)} %bitcast.8) | data formatting | bytes 33554432
  303.0 0.0 copy-done
  303.0 1.0 copy.20
  (6 shorter events, 0.0 us)
Async XLA Ops:
  288.7 14.3 %copy-start = (f32[2,1,256,512]{3,2,1,0:T(8,128)S(1)}, f32[2,1,256,512]{3,2,1,0:T(8,128)}, u32[]{:S(2)}) copy-start(f32[2,1,256,512]{3,2,1,0:T(8,128)} %get-tuple-element.17) | copy-start | bytes 3145732

commit v3 on v2

v3 whole, which is shorter than its diff:
```python
import math

import jax
import jax.numpy as jnp
from jax import lax
from jax.experimental import pallas as pl
from jax.experimental.pallas import tpu as pltpu
from jax.sharding import PartitionSpec as P

NORM_EPS = 1e-5
GROUP_EPS = 1e-6
ROPE_BASE = 10000.0
CHUNK = 256
BLOCKS = 4
CHIPS = 4
PARTS = 2
F32 = jnp.float32
BF16 = jnp.bfloat16
MESH = pl.DeviceIdType.MESH
LOOP = {
    0: (
        ('s1', 'e', 1, 0),
    ),
    1: (
        ('s1', 'e', 1, 1),
    ),
    2: (
        ('s1', 'e', 2, 0), ('s1', 'm', 'f1', 0), ('s1', 'm', 'f1', 1), ('s1', 'm', 'n1', 0), ('s1', 'm', 'n1', 1), ('s1', 'm', 'f2', 0),
    ),
    3: (
        ('rs', 'm', 0, 0, 'n'), ('s1', 'e', 2, 1),
    ),
    4: (
        ('s2', 'e', 1, 0), ('s1', 'm', 'f2', 1), ('s2', 'e', 2, 1), ('rs', 'm', 0, 1, 'n'), ('s2', 'e', 2, 0),
    ),
    5: (
        ('rs', 'm', 0, 0, 'f'), ('s1', 'e', 3, 0), ('s2', 'e', 1, 1), ('s3', 'e', 1, 0),
    ),
    6: (
        ('s3', 'e', 2, 1), ('rs', 'm', 1, 1, 'n'), ('s1', 'e', 3, 1), ('rs', 'm', 1, 0, 'n'), ('rs', 'm', 0, 1, 'f'),
        ('rs', 'm', 1, 1, 'f'),
    ),
}
BETWEEN = (
    ('rs', 'm', 2, 0, 'n'), ('s2', 'e', 3, 0), ('s2', 'e', 3, 1), ('rs', 'm', 1, 0, 'f'), ('fin', 'e', 0, 1), ('fin', 'e', 0, 0),
    ('rs', 'm', 3, 0, 'n'), ('s3', 'e', 1, 1), ('fin', 'e', 1, 1), ('rs', 'm', 2, 1, 'n'),
)
TILES = {
    2: (
        ('s3', 'e', 2, 0), ('s3', 'e', 3, 0),
    ),
    4: (
        ('s3', 'e', 3, 1), ('rs', 'm', 2, 0, 'f'),
    ),
    6: (
        ('rs', 'm', 3, 1, 'n'),
    ),
    7: (
        ('fin', 'e', 1, 0),
    ),
    9: (
        ('rs', 'm', 3, 0, 'f'), ('rs', 'm', 2, 1, 'f'),
    ),
    12: (
        ('ag', 'm', 'n', 0, 0),
    ),
    13: (
        ('fin', 'e', 3, 0),
    ),
    16: (
        ('fin', 'e', 2, 1), ('fin', 'e', 2, 0), ('rs', 'm', 3, 1, 'f'),
    ),
    18: (
        ('ag', 'm', 'n', 0, 1), ('ag', 'm', 'f', 0, 0), ('ag', 'm', 'n', 1, 0),
    ),
    19: (
        ('ag', 'm', 'f', 0, 1), ('ag', 'm', 'n', 1, 1), ('ag', 'm', 'f', 1, 0),
    ),
    20: (
        ('ag', 'm', 'n', 2, 0), ('ag', 'm', 'f', 1, 1), ('ag', 'm', 'n', 2, 1),
    ),
    23: (
        ('fin', 'e', 3, 1), ('ag', 'm', 'f', 2, 0), ('ag', 'm', 'n', 3, 0),
    ),
    25: (
        ('ag', 'e', 'x', 0, 0),
    ),
    27: (
        ('ag', 'm', 'f', 2, 1),
    ),
}
TAIL = (
    ('ag', 'm', 'n', 3, 1), ('ag', 'e', 'x', 2, 1), ('ag', 'e', 'x', 2, 0), ('ag', 'e', 'x', 1, 1), ('ag', 'm', 'f', 3, 0),
    ('ag', 'm', 'f', 3, 1), ('ag', 'e', 'x', 1, 0), ('ag', 'e', 'x', 3, 0), ('ag', 'e', 'x', 0, 1), ('ag', 'e', 'x', 3, 1),
)


def normalize(x_f32, gain, bias):
    row_mean = jnp.mean(x_f32, axis=-1, keepdims=True)
    centered = x_f32 - row_mean
    variance = jnp.mean(centered * centered, axis=-1, keepdims=True)
    return centered * lax.rsqrt(variance + NORM_EPS) * gain + bias


def add_bf16(*terms):
    return sum(t.astype(F32) for t in terms).astype(BF16)


def layer_kernel(x_any, state_in, gain1, bias1, gain2, bias2, wq_any, wk_any, wv_any, wg_any, wo_any, up_any, down_any, cos_high, sin_high, cos_low, sin_low,
                 out_any, state_ref, up_all, down_all,
                 wq, wk, wv, wg, wo, wd, x_buf, part, met, own, rs, mid, hid, acc, decay, edge,
                 load_sem, x_sem, mid_sem, tile_sem, met_s, met_r, credit, rs_s, rs_r, z_s, z_r, f_s, f_r, g_s, g_r, p_s, p_r, ag_s, ag_r, agp_s, agp_r, put_sem):
    group, me = lax.axis_index('dp'), lax.axis_index('tp')
    chip, core = lax.div(me, 2), lax.rem(me, 2)
    partner = me + 1 - 2 * core
    across_x = lax.rem(group + 2, 4)
    across_y = group + 1 - 2 * lax.rem(group, 2)
    chunk = cos_low.shape[0]
    rows, share = own.shape[1], mid.shape[1]
    key_dim, half = wq.shape[1], wq.shape[1] // 2
    last = CHIPS - 1
    far = 1 - 2 * lax.div(chip, 2)
    is_end = (chip == 0) | (chip == last)
    is_middle = (chip > 0) & (chip < last)

    def remote(src, dst, s, r, **where):
        return pltpu.make_async_remote_copy(src_ref=src, dst_ref=dst, send_sem=s, recv_sem=r, device_id=where, device_id_type=MESH)

    def side_of(flow):
        return lax.div(1 - flow, 2)

    shard = lax.div(chip, 2)
    weight_all, weight_own = (up_all, down_all), (up_any, down_any)
    quarter = tuple(w.shape[0] // 4 for w in weight_own)

    def origin_of(which):
        return {'n1': chip - far, 'f1': chip + far, 'f2': chip + 2 * far}[which] if isinstance(which, str) else chip + which * far

    def piece(p, index, q):
        return weight_all[p].at[index, pl.ds(q * quarter[p], quarter[p])]

    def z_copy(flow, origin, p, own_piece=False):
        slot = piece(p, 2 * origin + core, group)
        src = weight_own[p].at[pl.ds(group * quarter[p], quarter[p])] if own_piece else slot
        return remote(src, slot, z_s.at[side_of(flow), origin, p], z_r.at[origin, p], tp=me + 2 * flow)

    def first_copy(axis, origin, p, q=None):
        slot = piece(p, 2 * origin + core, group if q is None else q)
        return remote(slot, slot, f_s.at[axis, origin, p], f_r.at[axis, origin, p], dp=across_x if axis == 0 else across_y)

    def second_copy(origin, p, q=None):
        slot = piece(p, 2 * origin + core, (across_x if p == 0 else across_y) if q is None else q)
        return remote(slot, slot, g_s.at[origin, p], g_r.at[origin, p], dp=across_y if p == 0 else across_x)

    def partner_copy(origin, p, own_shard=False, incoming=False):
        slot = weight_all[p].at[2 * origin + (1 - core if incoming else core)]
        return remote(weight_own[p] if own_shard else slot, slot, p_s.at[origin, p], p_r.at[origin, p], tp=partner)

    def spread_first(which, p):
        origin = origin_of(which)
        z_copy(far, origin, p).wait_recv()
        if isinstance(which, str):
            z_copy(far if which == 'n1' else -far, origin, p).start()
        else:
            for axis in range(2):
                first_copy(axis, origin, p).start()

    def spread_second(which, p):
        origin = origin_of(which)
        first_copy(p, origin, p, across_x if p == 0 else across_y).wait_recv()
        second_copy(origin, p).start()

    def spread_third(which, p):
        origin = origin_of(which)
        first_copy(1 - p, origin, p, across_y if p == 0 else across_x).wait_recv()
        second_copy(origin, p, 3 - group).wait_recv()
        partner_copy(origin, p).start()

    def strip(h):
        return pl.ds(h * (share // PARTS), share // PARTS)

    def mine(i, h, side):
        return own[i, pl.ds(pl.multiple_of((1 - side) * share + h * (share // PARTS), share // PARTS), share // PARTS)]

    def rs_copy(flow, i, h, fresh=False):
        side = side_of(flow)
        slot = rs.at[side, i, strip(h)]
        src = own.at[i, pl.ds((1 - side) * share + h * (share // PARTS), share // PARTS)] if fresh else slot
        return remote(src, slot, rs_s.at[side, i, h], rs_r.at[side, i, h], tp=me + 2 * flow)

    def rs_first(i):
        @pl.when(is_end)
        def _():
            for h in range(PARTS):
                rs_copy(far, i, h, fresh=True).start()

    def rs_step(i, h, which):
        flow = far if which == 'n' else -far
        side = side_of(flow)
        rs_copy(flow, i, h).wait_recv()
        rs[side, i, strip(h)] = add_bf16(rs[side, i, strip(h)], mine(i, h, side))
        rs_copy(flow, i, h).start()

    def rs_final(i, h):
        side = side_of(-far)
        rs_copy(-far, i, h).wait_recv()
        mid[i, strip(h)] = add_bf16(mid[i, strip(h)], add_bf16(mine(i, h, side), rs[side, i, strip(h)]))

    def ag_copy(b, h, origin, fresh=False):
        slot = out_any.at[core, b, origin, strip(h)]
        return remote(mid.at[b, strip(h)] if fresh else slot, slot, ag_s.at[b, h, origin], ag_r.at[b, h, origin], tp=me + 2 * (1 - 2 * origin))

    def agp_copy(b, h, origin, fresh=False, incoming=False):
        slot = out_any.at[1 - core if incoming else core, b, origin, strip(h)]
        return remote(mid.at[b, strip(h)] if fresh else slot, slot, agp_s.at[b, h, origin], agp_r.at[b, h, origin], tp=partner)

    def put_copy(b):
        return pltpu.make_async_copy(mid.at[b], out_any.at[core, b, shard], put_sem.at[b])

    def ag_first(b):
        for h in range(PARTS):
            ag_copy(b, h, shard, fresh=True).start()
        for h in range(PARTS):
            agp_copy(b, h, shard, fresh=True).start()
        put_copy(b).start()

    def ag_step(which, b, h):
        origin = shard if which == 'n' else 1 - shard
        ag_copy(b, h, origin).wait_recv()
        if which != 'x':
            ag_copy(b, h, origin).start()
        agp_copy(b, h, origin).start()

    serves = {'s1': spread_first, 's2': spread_second, 's3': spread_third, 'rs': rs_step, 'fin': rs_final, 'ag': ag_step}

    def serve(items):
        for item in items:
            @pl.when(is_end if item[1] == 'e' else is_middle)
            def _():
                serves[item[0]](*item[2:])

    def x_copy(n):
        seq = core + (1 - 2 * core) * (1 - lax.rem(n, 2))
        return pltpu.make_async_copy(x_any.at[seq, lax.div(n, 2)], x_buf.at[lax.rem(n, 2)], x_sem.at[lax.rem(n, 2)])

    def met_copy(i):
        return remote(part, met.at[lax.rem(i, 2)], met_s, met_r.at[lax.rem(i, 2)], tp=partner)

    barrier = pltpu.get_barrier_semaphore()
    for where in ({'tp': partner}, {'dp': across_x}, {'dp': across_y}):
        pl.semaphore_signal(barrier, inc=1, device_id=where, device_id_type=MESH)

    @pl.when(chip < last)
    def _():
        pl.semaphore_signal(barrier, inc=1, device_id={'tp': me + 2}, device_id_type=MESH)

    @pl.when(chip > 0)
    def _():
        pl.semaphore_signal(barrier, inc=1, device_id={'tp': me - 2}, device_id_type=MESH)

    loads = [pltpu.make_async_copy(a, b, load_sem.at[k]) for k, (a, b) in enumerate(((wq_any, wq), (wk_any, wk), (wv_any, wv), (wg_any, wg), (wo_any, wo)))]
    x_copy(0).start()
    for load in loads:
        load.start()
    mid_load = pltpu.make_async_copy(x_any.at[core, :, shard], mid, mid_sem)
    mid_load.start()
    pl.semaphore_wait(barrier, 4 + is_middle.astype(jnp.int32))

    for p in range(2):
        z_copy(far, chip, p, own_piece=True).start()

        @pl.when(is_middle)
        def _():
            z_copy(-far, chip, p, own_piece=True).start()

        @pl.when(is_end)
        def _():
            partner_copy(chip, p, own_shard=True).start()

    state_ref[...] = state_in[...]
    log_gamma = F32(0.0)
    for head in range(2 * CHIPS):
        log_gamma = jnp.where(me == head, F32(math.log1p(-2.0 ** (-5 - head))), log_gamma)
    gap = lax.broadcasted_iota(jnp.int32, (chunk, chunk), 0) - lax.broadcasted_iota(jnp.int32, (chunk, chunk), 1)
    decay[...] = jnp.where(gap >= 0, jnp.exp(jnp.maximum(gap, 0).astype(F32) * log_gamma), 0.0)
    lane = lax.broadcasted_iota(jnp.int32, edge.shape, 1)
    ids = lax.broadcasted_iota(jnp.int32, edge.shape, 0)
    power = jnp.where(lane == 0, ids + 1, jnp.where(lane == 1, chunk - 1 - ids, chunk))
    edge[...] = jnp.exp(power.astype(F32) * log_gamma)
    for load in loads:
        load.wait()
    mid_load.wait()

    def attend(n, carry):
        i, k = lax.div(n, 2), lax.rem(n, 2)
        seq = core + (1 - 2 * core) * (1 - k)
        x_copy(n).wait()

        @pl.when(n < 2 * BLOCKS - 1)
        def _():
            x_copy(n + 1).start()

        h = normalize(x_buf[k].reshape(rows, part.shape[1]).astype(F32), gain1[...], bias1[...]).astype(BF16)
        q_raw = jnp.dot(h, wq[...], preferred_element_type=F32)
        k_raw = jnp.dot(h, wk[...], preferred_element_type=F32)
        v_all = jnp.dot(h, wv[...], preferred_element_type=F32).astype(BF16)
        g_all = jnp.dot(h, wg[...], preferred_element_type=F32)
        cos_lo, sin_lo = cos_low[...], sin_low[...]
        mixed = []
        subs = rows // chunk
        for sub in range(subs):
            span = slice(sub * chunk, (sub + 1) * chunk)
            row = pl.ds(i * subs + sub, 1)
            cos_hi, sin_hi = cos_high[seq, row, :], sin_high[seq, row, :]
            cos_t = cos_hi * cos_lo - sin_hi * sin_lo
            sin_t = sin_hi * cos_lo + cos_hi * sin_lo

            def rotate(raw):
                first, second = raw[span, :half], raw[span, half:]
                return jnp.concatenate([first * cos_t - second * sin_t, second * cos_t + first * sin_t], axis=-1)

            queries = rotate(q_raw).astype(BF16)
            keys = (rotate(k_raw) * key_dim ** -0.5).astype(BF16)
            values = v_all[span]
            state = state_ref[seq, 0]
            scores = lax.dot_general(queries, keys, (((1,), (1,)), ((), ())), preferred_element_type=F32) * decay[...]
            retained = jnp.dot(scores.astype(BF16), values, preferred_element_type=F32)
            retained += jnp.dot(queries, state.astype(BF16), preferred_element_type=F32) * edge[:, 0:1]
            keys_decayed = (keys.astype(F32) * edge[:, 1:2]).astype(BF16)
            grown = lax.dot_general(keys_decayed, values, (((0,), (0,)), ((), ())), preferred_element_type=F32)
            state_ref[seq, 0] = state * edge[0:1, 2:3] + grown
            row_mean = jnp.mean(retained, axis=-1, keepdims=True)
            centered = retained - row_mean
            variance = jnp.mean(centered * centered, axis=-1, keepdims=True)
            normed = centered * lax.rsqrt(variance + GROUP_EPS)
            mixed.append((jax.nn.silu(g_all[span]) * normed).astype(BF16))
        u = jnp.dot(jnp.concatenate(mixed, axis=0), wo[...], preferred_element_type=F32).astype(BF16)

        @pl.when(k == 1)
        def _():
            met_copy(i).wait_send()

        part[...] = u

        @pl.when(k == 0)
        def _():
            @pl.when(i >= 2)
            def _():
                pl.semaphore_wait(credit, 1)

            met_copy(i).start()

        @pl.when(k == 1)
        def _():
            met_copy(i).wait_recv()
            own[i] = add_bf16(part[...], met[lax.rem(i, 2)])

            @pl.when(i < BLOCKS - 2)
            def _():
                pl.semaphore_signal(credit, inc=1, device_id={'tp': partner}, device_id_type=MESH)

            rs_first(i)

        for turn, items in LOOP.items():
            @pl.when(n == turn)
            def _():
                serve(items)

        return carry

    lax.fori_loop(0, 2 * BLOCKS, attend, 0)

    serve(BETWEEN)

    slots = ((wv, wo), (wg, wd))

    def tile_copies(index, slot, own_shard=False):
        sources = (up_any, down_any) if own_shard else (up_all.at[index], down_all.at[index])
        return [pltpu.make_async_copy(sources[p], slots[slot][p], tile_sem.at[slot, p]) for p in range(2)]

    def ffn_tile(slot):
        for copy in tile_copies(0, slot):
            copy.wait()
        up, down = slots[slot]
        pre = jnp.dot(hid[...], up[...], preferred_element_type=F32)
        act = (0.5 * pre * (1.0 + lax.erf(pre * 0.5 ** 0.5))).astype(BF16)
        acc[...] += jnp.dot(act, down[...], preferred_element_type=F32)

    def ffn_finish(b):
        mid[b] = add_bf16(mid[b], acc[...].astype(BF16))
        ag_first(b)

    def serve_at(pair, parity, fresh):
        for turn, items in TILES.items():
            if turn % 2 == parity and (turn % 8 == 0) == fresh:
                @pl.when(pair == turn // 2)
                def _():
                    serve(items)

    def ffn_pair(pair, carry):
        b, e = lax.div(pair, CHIPS), lax.rem(pair, CHIPS)
        index = 2 * (chip + e * far) + core
        serve_at(pair, 0, False)

        @pl.when(is_end)
        def _():
            @pl.when(e == 0)
            def _():
                for copy in tile_copies(index, 0, own_shard=True):
                    copy.start()

            @pl.when(e > 0)
            def _():
                for copy in tile_copies(index, 0):
                    copy.start()

            @pl.when(pair > 0)
            def _():
                ffn_tile(1)

                @pl.when(e == 0)
                def _():
                    ffn_finish(b - 1)

        serve_at(pair, 0, True)

        @pl.when(is_end & (e == 0))
        def _():
            hid[...] = normalize(mid[b].astype(F32), gain2[...], bias2[...]).astype(BF16)
            acc[...] = jnp.zeros_like(acc)

        serve_at(pair, 1, False)

        @pl.when(is_end)
        def _():
            @pl.when(b == 0)
            def _():
                for p in range(2):
                    partner_copy(chip + e * far, p, incoming=True).wait_recv()

            for copy in tile_copies(index + 1 - 2 * core, 1):
                copy.start()
            ffn_tile(0)

        return carry

    lax.fori_loop(0, BLOCKS * CHIPS, ffn_pair, 0)

    @pl.when(is_end)
    def _():
        ffn_tile(1)
        ffn_finish(BLOCKS - 1)

    serve(TAIL)

    strips = [(b, h) for b in range(BLOCKS) for h in range(PARTS)]
    for b, h in strips:
        for origin in range(2):
            agp_copy(b, h, origin).wait_send()
            agp_copy(b, h, origin, incoming=True).wait_recv()
    for p in range(2):
        z_copy(far, chip, p).wait_send()

    @pl.when(is_end)
    def _():
        for b in range(BLOCKS):
            put_copy(b).wait()
        for b, h in strips:
            ag_copy(b, h, shard).wait_send()
            rs_copy(far, b, h, fresh=True).wait_send()
        for p in range(2):
            partner_copy(chip, p, own_shard=True).wait_send()
            for which in range(1, CHIPS):
                origin = origin_of(which)
                partner_copy(origin, p).wait_send()
                second_copy(origin, p).wait_send()
                for axis in range(2):
                    first_copy(axis, origin, p).wait_send()

    @pl.when(is_middle)
    def _():
        for p in range(2):
            z_copy(-far, chip, p).wait_send()
            z_copy(far, origin_of('n1'), p).wait_send()
            z_copy(-far, origin_of('f1'), p).wait_send()
            z_copy(-far, origin_of('f2'), p).wait_send()
        for b, h in strips:
            for side in range(2):
                rs_copy(1 - 2 * side, b, h).wait_send()
                ag_copy(b, h, side).wait_send()


def copy_kernel(a_ref, b_ref, a_out, b_out):
    a_out[...] = a_ref[...]
    b_out[...] = b_ref[...]


def copy_out(a, b):
    spec = pl.BlockSpec((1, a.shape[1] // 2) + a.shape[2:], lambda i: (i // 2, i % 2, 0))
    part = pl.BlockSpec((1, 1, b.shape[2] // 2, b.shape[3]), lambda i: (i // 2, 0, i % 2, 0))
    return pl.pallas_call(
        copy_kernel,
        grid=(2 * a.shape[0],),
        in_specs=[spec, part],
        out_specs=[spec, part],
        out_shape=[jax.ShapeDtypeStruct(a.shape, a.dtype), jax.ShapeDtypeStruct(b.shape, b.dtype)],
        compiler_params=pltpu.CompilerParams(vmem_limit_bytes=48 * 2 ** 20),
        name="copy_out",
    )(a, b)


def solution(mesh):
    members = mesh.shape['tp']

    def local_layer(x_in, start_pos, kv_state, ln1_gain, ln1_bias, w_q, w_k, w_v, w_g, w_o, ln2_gain, ln2_bias, w_up, w_down):
        seqs, chunk_len, d_model = x_in.shape
        key_dim = kv_state.shape[2]
        half = key_dim // 2
        rows = chunk_len // BLOCKS
        share = rows // 2
        chunk = min(CHUNK, rows)
        inv_freq = jnp.power(ROPE_BASE, -jnp.arange(half).astype(F32) / half)
        low = jnp.arange(chunk).astype(F32)[:, None] * inv_freq[None, :]
        high = (start_pos[:, None] + jnp.arange(chunk_len // chunk)[None, :] * chunk).astype(F32)[:, :, None] * inv_freq

        anywhere = pl.BlockSpec(memory_space=pl.ANY)
        vmem = pl.BlockSpec(memory_space=pltpu.VMEM)
        dma = lambda *shape: pltpu.SemaphoreType.DMA(shape)
        out, state, _, _ = pl.pallas_call(
            layer_kernel,
            in_specs=[anywhere, vmem, vmem, vmem, vmem, vmem] + [anywhere] * 7 + [vmem] * 4,
            out_specs=[anywhere, vmem, anywhere, anywhere],
            out_shape=[
                jax.ShapeDtypeStruct((seqs, BLOCKS, 2, share, d_model), BF16),
                jax.ShapeDtypeStruct(kv_state.shape, F32),
                jax.ShapeDtypeStruct((members,) + w_up.shape, BF16),
                jax.ShapeDtypeStruct((members,) + w_down.shape, BF16),
            ],
            scratch_shapes=[
                pltpu.VMEM(w_q.shape, BF16), pltpu.VMEM(w_k.shape, BF16), pltpu.VMEM(w_v.shape, BF16), pltpu.VMEM(w_g.shape, BF16),
                pltpu.VMEM(w_o.shape, BF16), pltpu.VMEM(w_down.shape, BF16),
                pltpu.VMEM((2, 2, share, d_model), BF16), pltpu.VMEM((rows, d_model), BF16), pltpu.VMEM((2, rows, d_model), BF16),
                pltpu.VMEM((BLOCKS, rows, d_model), BF16), pltpu.VMEM((2, BLOCKS, share, d_model), BF16),
                pltpu.VMEM((BLOCKS, share, d_model), BF16), pltpu.VMEM((share, d_model), BF16), pltpu.VMEM((share, d_model), F32),
                pltpu.VMEM((chunk, chunk), F32), pltpu.VMEM((chunk, 128), F32),
                dma(5), dma(2), pltpu.SemaphoreType.DMA, dma(2, 2), pltpu.SemaphoreType.DMA, dma(2), pltpu.SemaphoreType.REGULAR,
                dma(2, BLOCKS, PARTS), dma(2, BLOCKS, PARTS), dma(2, 4, 2), dma(4, 2), dma(2, 4, 2), dma(2, 4, 2), dma(4, 2), dma(4, 2), dma(4, 2), dma(4, 2),
                dma(BLOCKS, PARTS, 2), dma(BLOCKS, PARTS, 2), dma(BLOCKS, PARTS, 2), dma(BLOCKS, PARTS, 2), dma(BLOCKS),
            ],
            compiler_params=pltpu.CompilerParams(collective_id=0, has_side_effects=True, vmem_limit_bytes=67043328),
            name="layer",
        )(x_in.reshape(seqs, BLOCKS, 2, share, d_model), kv_state, *(a[None, :] for a in (ln1_gain, ln1_bias, ln2_gain, ln2_bias)), w_q, w_k, w_v, w_g, w_o, w_up, w_down, jnp.cos(high), jnp.sin(high), jnp.cos(low), jnp.sin(low))
        return copy_out(out.reshape(seqs, chunk_len, d_model), state)

    in_specs = (P('dp', None, None), P('dp'), P('dp', 'tp', None, None), P(), P(), P(None, 'tp'), P(None, 'tp'), P(None, 'tp'), P(None, 'tp'), P('tp', None), P(), P(), P(None, 'tp'), P('tp', None))
    out_specs = (P('dp', None, None), P('dp', 'tp', None, None))
    return jax.shard_map(local_layer, mesh=mesh, in_specs=in_specs, out_specs=out_specs, check_vma=False)
```

time: 304 us -> 276 us (0.908)
  local copies, waits for them, and re-layouts: 15.2 us -> 1.22 us
  Pallas kernels: 283 us -> 271 us
    pallas_call x1, Pallas kernels: 283 us -> 260 us  [local_layer(): pl.pallas_call(layer_kernel, in_specs=[anywhere, vmem, vmem, vmem, vmem,...]
    unnamed x4 -> x2, local copies, waits for them, and re-layouts: 15.2 us -> 1.22 us
    pallas_call x0 -> x1, Pallas kernels: none -> 11.6 us  [copy_out(): pl.pallas_call(copy_kernel, grid=(2 * a.shape[0],), in_specs=[spec, part]...]
where the time goes in v3:
time: 276 us
  Pallas kernels  271 us (98%)
    pallas_call x1, Pallas kernels, local_layer(): pl.pallas_call(layer_kernel, in_specs=[anywhere, vmem, vmem, vmem, vmem,...  260 us
    pallas_call x1, Pallas kernels, copy_out(): pl.pallas_call(copy_kernel, grid=(2 * a.shape[0],), in_specs=[spec, part]...  11.6 us

profile of v3, /device:TPU:0, one launch (start us, length us, event | category | flops | bytes accessed | tf_op | source)
XLA Modules:
  0.0 276.0 jit_solution(14964599967217304130)
XLA Ops:
  0.7 0.7 add_convert_fusion
  1.4 0.7 multiply_sine_fusion.1
  2.1 1.2 multiply_sine_fusion
  3.3 259.9 %layer.1 = (bf16[2,4,2,256,2048]{4,3,2,1,0:T(8,128)(2,1)}, f32[2,1,256,512]{3,2,1,0:T(8,128)}, bf16[8,2048,512]{2,1,0:T(8,128)(2,1)}, bf16[8,512,2048]{2,1,0:T(8,128)(2,1)}) custom-call(bf16[2,4,2,256,2048]{4,3,2,1,0:T(8,128)(2,1)} %bitcast.6, f32[2,1,256,512]{3,2,1,0:T(8,128)} %state_in.1, f32[1,2048]{1,0:T(1,128)} %bitcast.8, f32[1,2048]{1,0:T(1,128)} %bitcast.9, ...), custom_call_target="tpu_custom_call" | custom-call | tf_op jit(solution)/shard_map/layer/pallas_call | solution.py:529
  263.2 0.0 copy-start
  263.3 1.2 copy-done
  264.5 11.6 %copy_out.1 = (bf16[2,2048,2048]{2,1,0:T(8,128)(2,1)}, f32[2,1,256,512]{3,2,1,0:T(8,128)}) custom-call(bf16[2,2048,2048]{2,1,0:T(8,128)(2,1)} %bitcast.7, f32[2,1,256,512]{3,2,1,0:T(8,128)S(1)} %copy-done), custom_call_target="tpu_custom_call" | custom-call | tf_op jit(solution)/shard_map/copy_out/pallas_call | solution.py:501
  (3 shorter events, 0.0 us)
Async XLA Ops:
  263.2 1.2 copy-start

commit v4 on v3

--- a/solution.py
+++ b/solution.py
@@ -11,6 +11,7 @@
 GROUP_EPS = 1e-6
 ROPE_BASE = 10000.0
 CHUNK = 256
+LOW = 16
 BLOCKS = 4
 CHIPS = 4
 PARTS = 2
@@ -106,17 +107,17 @@
     return sum(t.astype(F32) for t in terms).astype(BF16)
 
 
-def layer_kernel(x_any, state_in, gain1, bias1, gain2, bias2, wq_any, wk_any, wv_any, wg_any, wo_any, up_any, down_any, cos_high, sin_high, cos_low, sin_low,
+def layer_kernel(x_any, state_in, gain1, bias1, gain2, bias2, wq_any, wk_any, wv_any, wg_any, wo_any, up_any, down_any, cos_rows, sin_rows,
                  out_any, state_ref, up_all, down_all,
-                 wq, wk, wv, wg, wo, wd, x_buf, part, met, own, rs, mid, hid, acc, decay, edge,
-                 load_sem, x_sem, mid_sem, tile_sem, met_s, met_r, credit, rs_s, rs_r, z_s, z_r, f_s, f_r, g_s, g_r, p_s, p_r, ag_s, ag_r, agp_s, agp_r, put_sem):
+                 wq, wk, wv, wg, wo, x_buf, part, met, own, rs, hid, acc, decay, edge, cos_low, sin_low,
+                 load_sem, x_sem, mid_sem, state_sem, tile_sem, met_s, met_r, credit, rs_s, rs_r, z_s, z_r, f_s, f_r, g_s, g_r, p_s, p_r, ag_s, ag_r, agp_s, agp_r, put_sem):
     group, me = lax.axis_index('dp'), lax.axis_index('tp')
     chip, core = lax.div(me, 2), lax.rem(me, 2)
     partner = me + 1 - 2 * core
     across_x = lax.rem(group + 2, 4)
     across_y = group + 1 - 2 * lax.rem(group, 2)
-    chunk = cos_low.shape[0]
-    rows, share = own.shape[1], mid.shape[1]
+    chunk = decay.shape[0]
+    rows, share = own.shape[1], rs.shape[2]
     key_dim, half = wq.shape[1], wq.shape[1] // 2
     last = CHIPS - 1
     far = 1 - 2 * lax.div(chip, 2)
@@ -129,7 +130,7 @@
     def side_of(flow):
         return lax.div(1 - flow, 2)
 
-    shard = lax.div(chip, 2)
+    shard, kept = lax.div(chip, 2), side_of(far)
     weight_all, weight_own = (up_all, down_all), (up_any, down_any)
     quarter = tuple(w.shape[0] // 4 for w in weight_own)
 
@@ -204,18 +205,18 @@
     def rs_final(i, h):
         side = side_of(-far)
         rs_copy(-far, i, h).wait_recv()
-        mid[i, strip(h)] = add_bf16(mid[i, strip(h)], add_bf16(mine(i, h, side), rs[side, i, strip(h)]))
+        rs[kept, i, strip(h)] = add_bf16(rs[kept, i, strip(h)], add_bf16(mine(i, h, side), rs[side, i, strip(h)]))
 
     def ag_copy(b, h, origin, fresh=False):
         slot = out_any.at[core, b, origin, strip(h)]
-        return remote(mid.at[b, strip(h)] if fresh else slot, slot, ag_s.at[b, h, origin], ag_r.at[b, h, origin], tp=me + 2 * (1 - 2 * origin))
+        return remote(rs.at[kept, b, strip(h)] if fresh else slot, slot, ag_s.at[b, h, origin], ag_r.at[b, h, origin], tp=me + 2 * (1 - 2 * origin))
 
     def agp_copy(b, h, origin, fresh=False, incoming=False):
         slot = out_any.at[1 - core if incoming else core, b, origin, strip(h)]
-        return remote(mid.at[b, strip(h)] if fresh else slot, slot, agp_s.at[b, h, origin], agp_r.at[b, h, origin], tp=partner)
+        return remote(rs.at[kept, b, strip(h)] if fresh else slot, slot, agp_s.at[b, h, origin], agp_r.at[b, h, origin], tp=partner)
 
     def put_copy(b):
-        return pltpu.make_async_copy(mid.at[b], out_any.at[core, b, shard], put_sem.at[b])
+        return pltpu.make_async_copy(rs.at[kept, b], out_any.at[core, b, shard], put_sem.at[b])
 
     def ag_first(b):
         for h in range(PARTS):
@@ -241,10 +242,10 @@
 
     def x_copy(n):
         seq = core + (1 - 2 * core) * (1 - lax.rem(n, 2))
-        return pltpu.make_async_copy(x_any.at[seq, lax.div(n, 2)], x_buf.at[lax.rem(n, 2)], x_sem.at[lax.rem(n, 2)])
-
-    def met_copy(i):
-        return remote(part, met.at[lax.rem(i, 2)], met_s, met_r.at[lax.rem(i, 2)], tp=partner)
+        return pltpu.make_async_copy(x_any.at[seq, lax.div(n, 2)], x_buf, x_sem)
+
+    def met_copy():
+        return remote(part, met, met_s, met_r, tp=partner)
 
     barrier = pltpu.get_barrier_semaphore()
     for where in ({'tp': partner}, {'dp': across_x}, {'dp': across_y}):
@@ -262,8 +263,14 @@
     x_copy(0).start()
     for load in loads:
         load.start()
-    mid_load = pltpu.make_async_copy(x_any.at[core, :, shard], mid, mid_sem)
-    mid_load.start()
+    state_load = pltpu.make_async_copy(state_in, state_ref, state_sem)
+    state_load.start()
+    mid_load = pltpu.make_async_copy(x_any.at[core, :, shard], rs.at[kept], mid_sem)
+
+    @pl.when(is_end)
+    def _():
+        mid_load.start()
+
     pl.semaphore_wait(barrier, 4 + is_middle.astype(jnp.int32))
 
     for p in range(2):
@@ -277,7 +284,6 @@
         def _():
             partner_copy(chip, p, own_shard=True).start()
 
-    state_ref[...] = state_in[...]
     log_gamma = F32(0.0)
     for head in range(2 * CHIPS):
         log_gamma = jnp.where(me == head, F32(math.log1p(-2.0 ** (-5 - head))), log_gamma)
@@ -287,20 +293,31 @@
     ids = lax.broadcasted_iota(jnp.int32, edge.shape, 0)
     power = jnp.where(lane == 0, ids + 1, jnp.where(lane == 1, chunk - 1 - ids, chunk))
     edge[...] = jnp.exp(power.astype(F32) * log_gamma)
+    for group_row in range(chunk // LOW):
+        row, span = slice(cos_rows.shape[0] - LOW - chunk // LOW + group_row, cos_rows.shape[0] - LOW - chunk // LOW + group_row + 1), slice(group_row * LOW, (group_row + 1) * LOW)
+        cos_a, sin_a, cos_b, sin_b = cos_rows[row, :], sin_rows[row, :], cos_rows[cos_rows.shape[0] - LOW:, :], sin_rows[cos_rows.shape[0] - LOW:, :]
+        cos_low[span, :] = cos_a * cos_b - sin_a * sin_b
+        sin_low[span, :] = sin_a * cos_b + cos_a * sin_b
     for load in loads:
         load.wait()
-    mid_load.wait()
+    state_load.wait()
+
+    @pl.when(is_end)
+    def _():
+        mid_load.wait()
+
 
     def attend(n, carry):
         i, k = lax.div(n, 2), lax.rem(n, 2)
         seq = core + (1 - 2 * core) * (1 - k)
         x_copy(n).wait()
 
+        h = normalize(x_buf[...].reshape(rows, part.shape[1]).astype(F32), gain1[...], bias1[...]).astype(BF16)
+
         @pl.when(n < 2 * BLOCKS - 1)
         def _():
             x_copy(n + 1).start()
 
-        h = normalize(x_buf[k].reshape(rows, part.shape[1]).astype(F32), gain1[...], bias1[...]).astype(BF16)
         q_raw = jnp.dot(h, wq[...], preferred_element_type=F32)
         k_raw = jnp.dot(h, wk[...], preferred_element_type=F32)
         v_all = jnp.dot(h, wv[...], preferred_element_type=F32).astype(BF16)
@@ -310,8 +327,8 @@
         subs = rows // chunk
         for sub in range(subs):
             span = slice(sub * chunk, (sub + 1) * chunk)
-            row = pl.ds(i * subs + sub, 1)
-            cos_hi, sin_hi = cos_high[seq, row, :], sin_high[seq, row, :]
+            row = pl.ds(seq * (BLOCKS * subs) + i * subs + sub, 1)
+            cos_hi, sin_hi = cos_rows[row, :], sin_rows[row, :]
             cos_t = cos_hi * cos_lo - sin_hi * sin_lo
             sin_t = sin_hi * cos_lo + cos_hi * sin_lo
 
@@ -338,24 +355,24 @@
 
         @pl.when(k == 1)
         def _():
-            met_copy(i).wait_send()
+            met_copy().wait_send()
 
         part[...] = u
 
         @pl.when(k == 0)
         def _():
-            @pl.when(i >= 2)
+            @pl.when(i >= 1)
             def _():
                 pl.semaphore_wait(credit, 1)
 
-            met_copy(i).start()
+            met_copy().start()
 
         @pl.when(k == 1)
         def _():
-            met_copy(i).wait_recv()
-            own[i] = add_bf16(part[...], met[lax.rem(i, 2)])
-
-            @pl.when(i < BLOCKS - 2)
+            met_copy().wait_recv()
+            own[i] = add_bf16(part[...], met[...])
+
+            @pl.when(i < BLOCKS - 1)
             def _():
                 pl.semaphore_signal(credit, inc=1, device_id={'tp': partner}, device_id_type=MESH)
 
@@ -372,7 +389,7 @@
 
     serve(BETWEEN)
 
-    slots = ((wv, wo), (wg, wd))
+    slots = ((wv, wo), (wg, part))
 
     def tile_copies(index, slot, own_shard=False):
         sources = (up_any, down_any) if own_shard else (up_all.at[index], down_all.at[index])
@@ -387,7 +404,7 @@
         acc[...] += jnp.dot(act, down[...], preferred_element_type=F32)
 
     def ffn_finish(b):
-        mid[b] = add_bf16(mid[b], acc[...].astype(BF16))
+        rs[kept, b] = add_bf16(rs[kept, b], acc[...].astype(BF16))
         ag_first(b)
 
     def serve_at(pair, parity, fresh):
@@ -426,7 +443,7 @@
 
         @pl.when(is_end & (e == 0))
         def _():
-            hid[...] = normalize(mid[b].astype(F32), gain2[...], bias2[...]).astype(BF16)
+            hid[...] = normalize(rs[kept, b].astype(F32), gain2[...], bias2[...]).astype(BF16)
             acc[...] = jnp.zeros_like(acc)
 
         serve_at(pair, 1, False)
@@ -490,25 +507,6 @@
                 ag_copy(b, h, side).wait_send()
 
 
-def copy_kernel(a_ref, b_ref, a_out, b_out):
-    a_out[...] = a_ref[...]
-    b_out[...] = b_ref[...]
-
-
-def copy_out(a, b):
-    spec = pl.BlockSpec((1, a.shape[1] // 2) + a.shape[2:], lambda i: (i // 2, i % 2, 0))
-    part = pl.BlockSpec((1, 1, b.shape[2] // 2, b.shape[3]), lambda i: (i // 2, 0, i % 2, 0))
-    return pl.pallas_call(
-        copy_kernel,
-        grid=(2 * a.shape[0],),
-        in_specs=[spec, part],
-        out_specs=[spec, part],
-        out_shape=[jax.ShapeDtypeStruct(a.shape, a.dtype), jax.ShapeDtypeStruct(b.shape, b.dtype)],
-        compiler_params=pltpu.CompilerParams(vmem_limit_bytes=48 * 2 ** 20),
-        name="copy_out",
-    )(a, b)
-
-
 def solution(mesh):
     members = mesh.shape['tp']
 
@@ -520,37 +518,40 @@
         share = rows // 2
         chunk = min(CHUNK, rows)
         inv_freq = jnp.power(ROPE_BASE, -jnp.arange(half).astype(F32) / half)
-        low = jnp.arange(chunk).astype(F32)[:, None] * inv_freq[None, :]
-        high = (start_pos[:, None] + jnp.arange(chunk_len // chunk)[None, :] * chunk).astype(F32)[:, :, None] * inv_freq
+        pieces = chunk_len // chunk
+        row = jnp.arange(seqs * pieces + chunk // LOW + LOW)
+        begin = jnp.where(row < pieces, start_pos[0], start_pos[1] - pieces * chunk)
+        position = jnp.where(row < seqs * pieces, begin + row * chunk, jnp.where(row < row.size - LOW, (row - seqs * pieces) * LOW, row - (row.size - LOW)))
+        angles = position.astype(F32)[:, None] * inv_freq[None, :]
 
         anywhere = pl.BlockSpec(memory_space=pl.ANY)
         vmem = pl.BlockSpec(memory_space=pltpu.VMEM)
         dma = lambda *shape: pltpu.SemaphoreType.DMA(shape)
         out, state, _, _ = pl.pallas_call(
             layer_kernel,
-            in_specs=[anywhere, vmem, vmem, vmem, vmem, vmem] + [anywhere] * 7 + [vmem] * 4,
+            in_specs=[anywhere, anywhere, vmem, vmem, vmem, vmem] + [anywhere] * 7 + [vmem] * 2,
             out_specs=[anywhere, vmem, anywhere, anywhere],
             out_shape=[
-                jax.ShapeDtypeStruct((seqs, BLOCKS, 2, share, d_model), BF16),
+                pltpu.VMEM((seqs, BLOCKS, 2, share, d_model), BF16),
                 jax.ShapeDtypeStruct(kv_state.shape, F32),
                 jax.ShapeDtypeStruct((members,) + w_up.shape, BF16),
                 jax.ShapeDtypeStruct((members,) + w_down.shape, BF16),
             ],
             scratch_shapes=[
                 pltpu.VMEM(w_q.shape, BF16), pltpu.VMEM(w_k.shape, BF16), pltpu.VMEM(w_v.shape, BF16), pltpu.VMEM(w_g.shape, BF16),
-                pltpu.VMEM(w_o.shape, BF16), pltpu.VMEM(w_down.shape, BF16),
-                pltpu.VMEM((2, 2, share, d_model), BF16), pltpu.VMEM((rows, d_model), BF16), pltpu.VMEM((2, rows, d_model), BF16),
+                pltpu.VMEM(w_o.shape, BF16),
+                pltpu.VMEM((2, share, d_model), BF16), pltpu.VMEM((rows, d_model), BF16), pltpu.VMEM((rows, d_model), BF16),
                 pltpu.VMEM((BLOCKS, rows, d_model), BF16), pltpu.VMEM((2, BLOCKS, share, d_model), BF16),
-                pltpu.VMEM((BLOCKS, share, d_model), BF16), pltpu.VMEM((share, d_model), BF16), pltpu.VMEM((share, d_model), F32),
-                pltpu.VMEM((chunk, chunk), F32), pltpu.VMEM((chunk, 128), F32),
-                dma(5), dma(2), pltpu.SemaphoreType.DMA, dma(2, 2), pltpu.SemaphoreType.DMA, dma(2), pltpu.SemaphoreType.REGULAR,
+                pltpu.VMEM((share, d_model), BF16), pltpu.VMEM((share, d_model), F32),
+                pltpu.VMEM((chunk, chunk), F32), pltpu.VMEM((chunk, 128), F32), pltpu.VMEM((chunk, half), F32), pltpu.VMEM((chunk, half), F32),
+                dma(5), pltpu.SemaphoreType.DMA, pltpu.SemaphoreType.DMA, pltpu.SemaphoreType.DMA, dma(2, 2), pltpu.SemaphoreType.DMA, pltpu.SemaphoreType.DMA, pltpu.SemaphoreType.REGULAR,
                 dma(2, BLOCKS, PARTS), dma(2, BLOCKS, PARTS), dma(2, 4, 2), dma(4, 2), dma(2, 4, 2), dma(2, 4, 2), dma(4, 2), dma(4, 2), dma(4, 2), dma(4, 2),
                 dma(BLOCKS, PARTS, 2), dma(BLOCKS, PARTS, 2), dma(BLOCKS, PARTS, 2), dma(BLOCKS, PARTS, 2), dma(BLOCKS),
             ],
-            compiler_params=pltpu.CompilerParams(collective_id=0, has_side_effects=True, vmem_limit_bytes=67043328),
+            compiler_params=pltpu.CompilerParams(collective_id=0, has_side_effects=True, vmem_limit_bytes=47 * 2 ** 20),
             name="layer",
-        )(x_in.reshape(seqs, BLOCKS, 2, share, d_model), kv_state, *(a[None, :] for a in (ln1_gain, ln1_bias, ln2_gain, ln2_bias)), w_q, w_k, w_v, w_g, w_o, w_up, w_down, jnp.cos(high), jnp.sin(high), jnp.cos(low), jnp.sin(low))
-        return copy_out(out.reshape(seqs, chunk_len, d_model), state)
+        )(x_in.reshape(seqs, BLOCKS, 2, share, d_model), kv_state, *(a[None, :] for a in (ln1_gain, ln1_bias, ln2_gain, ln2_bias)), w_q, w_k, w_v, w_g, w_o, w_up, w_down, jnp.cos(angles), jnp.sin(angles))
+        return out.reshape(seqs, chunk_len, d_model), state
 
     in_specs = (P('dp', None, None), P('dp'), P('dp', 'tp', None, None), P(), P(), P(None, 'tp'), P(None, 'tp'), P(None, 'tp'), P(None, 'tp'), P('tp', None), P(), P(), P(None, 'tp'), P('tp', None))
     out_specs = (P('dp', None, None), P('dp', 'tp', None, None))

time: 276 us -> 270 us (0.978)
  Pallas kernels: 271 us -> 259 us
  local copies, waits for them, and re-layouts: 1.22 us -> 8.45 us
    pallas_call x2 -> x1, Pallas kernels: 271 us -> 259 us  [local_layer(): pl.pallas_call(layer_kernel, in_specs=[anywhere, anywhere, vmem, vmem, vm...]
    unnamed x2 -> x4, local copies, waits for them, and re-layouts: 1.22 us -> 7.14 us
where the time goes in v4:
time: 270 us
  Pallas kernels  259 us (96%)
  local copies, waits for them, and re-layouts  8.45 us (3%)
    pallas_call x1, Pallas kernels, local_layer(): pl.pallas_call(layer_kernel, in_specs=[anywhere, anywhere, vmem, vmem, vm...  259 us
    unnamed x4, local copies, waits for them, and re-layouts  7.14 us

profile of v4, /device:TPU:0, one launch (start us, length us, event | category | flops | bytes accessed | tf_op | source)
XLA Modules:
  0.0 269.7 jit_solution(9672208713929798427)
XLA Ops:
  0.6 1.3 fusion.3
  2.6 0.7 fusion.2
  3.3 0.8 multiply_sine_fusion
  4.1 258.5 %layer.1 = (bf16[2,4,2,256,2048]{4,3,2,1,0:T(8,128)(2,1)S(1)}, f32[2,1,256,512]{3,2,1,0:T(8,128)}, bf16[8,2048,512]{2,1,0:T(8,128)(2,1)}, bf16[8,512,2048]{2,1,0:T(8,128)(2,1)}) custom-call(bf16[2,4,2,256,2048]{4,3,2,1,0:T(8,128)(2,1)} %bitcast.9, f32[2,1,256,512]{3,2,1,0:T(8,128)} %state_in.1, f32[1,2048]{1,0:T(1,128)} %bitcast.10, f32[1,2048]{1,0:T(1,128)} %bitcast.11, ...), custom_call_target="tpu_custom_call" | custom-call | tf_op jit(solution)/shard_map/layer/pallas_call | solution.py:530
  262.6 0.0 copy-start
  262.6 6.2 %copy.18 = bf16[2,2048,2048]{2,1,0:T(8,128)(2,1)} copy(bf16[2,2048,2048]{2,1,0:T(8,128)(2,1)S(1)} %bitcast.8) | data formatting | bytes 33554432
  268.8 0.0 copy-done
  268.8 1.0 copy.19
  (1 shorter events, 0.0 us)
Async XLA Ops:
  262.6 6.2 %copy-start = (f32[2,1,256,512]{3,2,1,0:T(8,128)S(1)}, f32[2,1,256,512]{3,2,1,0:T(8,128)}, u32[]{:S(2)}) copy-start(f32[2,1,256,512]{3,2,1,0:T(8,128)} %get-tuple-element.15) | copy-start | bytes 3145732

commit v5 on v4

--- a/solution.py
+++ b/solution.py
@@ -2,6 +2,7 @@
 
 import jax
 import jax.numpy as jnp
+import numpy as np
 from jax import lax
 from jax.experimental import pallas as pl
 from jax.experimental.pallas import tpu as pltpu
@@ -107,9 +108,9 @@
     return sum(t.astype(F32) for t in terms).astype(BF16)
 
 
-def layer_kernel(x_any, state_in, gain1, bias1, gain2, bias2, wq_any, wk_any, wv_any, wg_any, wo_any, up_any, down_any, cos_rows, sin_rows,
+def layer_kernel(x_any, state_in, gain1, bias1, gain2, bias2, wq_any, wk_any, wv_any, wg_any, wo_any, up_any, down_any, cos_first, sin_first, step_rows,
                  out_any, state_ref, up_all, down_all,
-                 wq, wk, wv, wg, wo, x_buf, part, met, own, rs, hid, acc, decay, edge, cos_low, sin_low,
+                 wq, wk, wv, wg, wo, x_buf, part, met, own, rs, hid, acc, decay, edge, cos_low, sin_low, cos_rows, sin_rows,
                  load_sem, x_sem, mid_sem, state_sem, tile_sem, met_s, met_r, credit, rs_s, rs_r, z_s, z_r, f_s, f_r, g_s, g_r, p_s, p_r, ag_s, ag_r, agp_s, agp_r, put_sem):
     group, me = lax.axis_index('dp'), lax.axis_index('tp')
     chip, core = lax.div(me, 2), lax.rem(me, 2)
@@ -293,11 +294,19 @@
     ids = lax.broadcasted_iota(jnp.int32, edge.shape, 0)
     power = jnp.where(lane == 0, ids + 1, jnp.where(lane == 1, chunk - 1 - ids, chunk))
     edge[...] = jnp.exp(power.astype(F32) * log_gamma)
-    for group_row in range(chunk // LOW):
-        row, span = slice(cos_rows.shape[0] - LOW - chunk // LOW + group_row, cos_rows.shape[0] - LOW - chunk // LOW + group_row + 1), slice(group_row * LOW, (group_row + 1) * LOW)
-        cos_a, sin_a, cos_b, sin_b = cos_rows[row, :], sin_rows[row, :], cos_rows[cos_rows.shape[0] - LOW:, :], sin_rows[cos_rows.shape[0] - LOW:, :]
+    turns = chunk // LOW
+    cos_b, sin_b = step_rows[0, turns:turns + LOW, :], step_rows[1, turns:turns + LOW, :]
+    for turn in range(turns):
+        span = slice(turn * LOW, (turn + 1) * LOW)
+        cos_a, sin_a = step_rows[0, turn:turn + 1, :], step_rows[1, turn:turn + 1, :]
         cos_low[span, :] = cos_a * cos_b - sin_a * sin_b
         sin_low[span, :] = sin_a * cos_b + cos_a * sin_b
+    cos_b, sin_b = step_rows[0, turns + LOW:, :], step_rows[1, turns + LOW:, :]
+    for seq in range(2):
+        span = slice(seq * cos_b.shape[0], (seq + 1) * cos_b.shape[0])
+        cos_a, sin_a = cos_first[seq:seq + 1, :], sin_first[seq:seq + 1, :]
+        cos_rows[span, :] = cos_a * cos_b - sin_a * sin_b
+        sin_rows[span, :] = sin_a * cos_b + cos_a * sin_b
     for load in loads:
         load.wait()
     state_load.wait()
@@ -517,19 +526,18 @@
         rows = chunk_len // BLOCKS
         share = rows // 2
         chunk = min(CHUNK, rows)
-        inv_freq = jnp.power(ROPE_BASE, -jnp.arange(half).astype(F32) / half)
-        pieces = chunk_len // chunk
-        row = jnp.arange(seqs * pieces + chunk // LOW + LOW)
-        begin = jnp.where(row < pieces, start_pos[0], start_pos[1] - pieces * chunk)
-        position = jnp.where(row < seqs * pieces, begin + row * chunk, jnp.where(row < row.size - LOW, (row - seqs * pieces) * LOW, row - (row.size - LOW)))
-        angles = position.astype(F32)[:, None] * inv_freq[None, :]
+        inv_freq = (ROPE_BASE ** (-np.arange(half) / half)).astype(np.float32)
+        angles = start_pos.astype(F32)[:, None] * inv_freq[None, :]
+        steps = np.concatenate([np.arange(0, chunk, LOW), np.arange(LOW), np.arange(0, chunk_len, chunk)])
+        turns = steps[:, None] * inv_freq.astype(np.float64)
+        step_rows = jnp.asarray(np.stack([np.cos(turns), np.sin(turns)]).astype(np.float32))
 
         anywhere = pl.BlockSpec(memory_space=pl.ANY)
         vmem = pl.BlockSpec(memory_space=pltpu.VMEM)
         dma = lambda *shape: pltpu.SemaphoreType.DMA(shape)
         out, state, _, _ = pl.pallas_call(
             layer_kernel,
-            in_specs=[anywhere, anywhere, vmem, vmem, vmem, vmem] + [anywhere] * 7 + [vmem] * 2,
+            in_specs=[anywhere, anywhere, vmem, vmem, vmem, vmem] + [anywhere] * 7 + [vmem] * 3,
             out_specs=[anywhere, vmem, anywhere, anywhere],
             out_shape=[
                 pltpu.VMEM((seqs, BLOCKS, 2, share, d_model), BF16),
@@ -543,14 +551,14 @@
                 pltpu.VMEM((2, share, d_model), BF16), pltpu.VMEM((rows, d_model), BF16), pltpu.VMEM((rows, d_model), BF16),
                 pltpu.VMEM((BLOCKS, rows, d_model), BF16), pltpu.VMEM((2, BLOCKS, share, d_model), BF16),
                 pltpu.VMEM((share, d_model), BF16), pltpu.VMEM((share, d_model), F32),
-                pltpu.VMEM((chunk, chunk), F32), pltpu.VMEM((chunk, 128), F32), pltpu.VMEM((chunk, half), F32), pltpu.VMEM((chunk, half), F32),
+                pltpu.VMEM((chunk, chunk), F32), pltpu.VMEM((chunk, 128), F32), *[pltpu.VMEM((count, half), F32) for count in (chunk, chunk, seqs * (chunk_len // chunk), seqs * (chunk_len // chunk))],
                 dma(5), pltpu.SemaphoreType.DMA, pltpu.SemaphoreType.DMA, pltpu.SemaphoreType.DMA, dma(2, 2), pltpu.SemaphoreType.DMA, pltpu.SemaphoreType.DMA, pltpu.SemaphoreType.REGULAR,
                 dma(2, BLOCKS, PARTS), dma(2, BLOCKS, PARTS), dma(2, 4, 2), dma(4, 2), dma(2, 4, 2), dma(2, 4, 2), dma(4, 2), dma(4, 2), dma(4, 2), dma(4, 2),
                 dma(BLOCKS, PARTS, 2), dma(BLOCKS, PARTS, 2), dma(BLOCKS, PARTS, 2), dma(BLOCKS, PARTS, 2), dma(BLOCKS),
             ],
             compiler_params=pltpu.CompilerParams(collective_id=0, has_side_effects=True, vmem_limit_bytes=47 * 2 ** 20),
             name="layer",
-        )(x_in.reshape(seqs, BLOCKS, 2, share, d_model), kv_state, *(a[None, :] for a in (ln1_gain, ln1_bias, ln2_gain, ln2_bias)), w_q, w_k, w_v, w_g, w_o, w_up, w_down, jnp.cos(angles), jnp.sin(angles))
+        )(x_in.reshape(seqs, BLOCKS, 2, share, d_model), kv_state, *(a[None, :] for a in (ln1_gain, ln1_bias, ln2_gain, ln2_bias)), w_q, w_k, w_v, w_g, w_o, w_up, w_down, jnp.cos(angles), jnp.sin(angles), step_rows)
         return out.reshape(seqs, chunk_len, d_model), state
 
     in_specs = (P('dp', None, None), P('dp'), P('dp', 'tp', None, None), P(), P(), P(None, 'tp'), P(None, 'tp'), P(None, 'tp'), P(None, 'tp'), P('tp', None), P(), P(), P(None, 'tp'), P('tp', None))

time: 270 us -> 269 us (level)
  no operation moved by 1% of the time
where the time goes in v5:
time: 269 us; the launch traced here: 268 us
  Pallas kernels  259 us (96%)
  local copies, waits for them, and re-layouts  7.14 us (3%)
    pallas_call x1, Pallas kernels, local_layer(): pl.pallas_call(layer_kernel, in_specs=[anywhere, anywhere, vmem, vmem, vm...  259 us
    unnamed x4, local copies, waits for them, and re-layouts  7.14 us

profile of v5, /device:TPU:0, one launch (start us, length us, event | category | flops | bytes accessed | tf_op | source)
XLA Modules:
  0.0 268.5 jit_solution(8243353164347502600)
XLA Ops:
  0.6 0.7 convert_element_type.3
  1.3 1.3 multiply_sine_fusion
  2.6 258.7 %layer.1 = (bf16[2,4,2,256,2048]{4,3,2,1,0:T(8,128)(2,1)S(1)}, f32[2,1,256,512]{3,2,1,0:T(8,128)}, bf16[8,2048,512]{2,1,0:T(8,128)(2,1)}, bf16[8,512,2048]{2,1,0:T(8,128)(2,1)}) custom-call(bf16[2,4,2,256,2048]{4,3,2,1,0:T(8,128)(2,1)} %bitcast.7, f32[2,1,256,512]{3,2,1,0:T(8,128)} %state_in.1, f32[1,2048]{1,0:T(1,128)} %bitcast.8, f32[1,2048]{1,0:T(1,128)} %bitcast.9, ...), custom_call_target="tpu_custom_call" | custom-call | tf_op jit(solution)/shard_map/layer/pallas_call | solution.py:538
  261.3 0.0 copy-start
  261.3 6.2 %copy.20 = bf16[2,2048,2048]{2,1,0:T(8,128)(2,1)} copy(bf16[2,2048,2048]{2,1,0:T(8,128)(2,1)S(1)} %bitcast.6) | data formatting | bytes 33554432
  267.5 0.0 copy-done
  267.5 1.0 copy.21
Async XLA Ops:
  261.3 6.2 %copy-start = (f32[2,1,256,512]{3,2,1,0:T(8,128)S(1)}, f32[2,1,256,512]{3,2,1,0:T(8,128)}, u32[]{:S(2)}) copy-start(f32[2,1,256,512]{3,2,1,0:T(8,128)} %get-tuple-element.13) | copy-start | bytes 3145732
